TPU v7x, 512 devices: a whole 4x8x8 slice. The times are simulated.
512 devices in a mesh: dp: 256 (over y, z_hi, x, core), mp: 2 (over z_lo).
Axes of the slice: x: 4, y: 8, z: 8 (z_hi: 4, z_lo: 2; z = z_hi * 2 + z_lo), core: 2. Of those that a mesh axis runs over, the one named last changes fastest.
Arguments:
- new_embed: bfloat16 [28672, 1280], P('dp'), may hold values from -3 to 3
- context_key_cache: bfloat16 [28672, 16, 1280], P('dp', None, 'mp'), may hold values from -2500 to 2500
- value_cache: bfloat16 [28672, 16, 1280], P('dp', None, 'mp'), may hold values from -6 to 6
- valid: int32 [28672], P('dp'), may hold values from 2 to 16
- attn_gain: float32 [1280], replicated, may hold values from 0.1 to 1.9
- mlp_gain: float32 [1280], replicated, may hold values from 0.1 to 1.9
- query_scale: float32 [80], replicated, may hold values from 0.1 to 1.9
- w_qkv: bfloat16 [3, 1280, 1280], P(None, 'dp', 'mp'), may hold values from -0.15625 to 0.15625
- w_out: bfloat16 [1280, 1280], P('mp', 'dp'), may hold values from -0.625 to 0.625
- w_up: bfloat16 [1280, 1280], P('dp', 'mp'), may hold values from -0.15625 to 0.15625
- w_down: bfloat16 [1280, 1280], P('mp', 'dp'), may hold values from -0.15625 to 0.15625
- head_hidden: bfloat16 [1280, 1280], P('dp', 'mp'), may hold values from -0.15625 to 0.15625
- final_layer_matrices: bfloat16 [2, 1280, 1280], P(None, 'mp', 'dp'), may hold values from -0.15625 to 0.15625
Outputs:
- predicted_levels: float32 [28672, 1280], P('dp', 'mp')
Inputs may be any that keep to these rules, and one draw needn't show every extreme that they name: Series s uses its first valid[s] cached patches.
All inputs are finite; a program needn't handle non-finite values.
Results may differ from a plain program's by a relative error of at most 0.035.
Values may be sent and summed in bfloat16 or wider, within the bound.
No kernel may reach another device: no remote copies, remote signals or barrier semaphores. Data moves between devices by JAX's collectives and lax.ppermute only.
A program may use at most 128 MiB of HBM per device.

v0:
```python
import math

import jax
import jax.numpy as jnp
import numpy as np
from jax import lax
from jax.experimental import pallas as pl
from jax.experimental.pallas import tpu as pltpu
from jax.sharding import Mesh
from jax.sharding import PartitionSpec as P

D = 1280
HEADS = 16
HD = D // HEADS
DP = ("y", "zh", "x", "c")
NY, NZ, NX, NC = 8, 4, 4, 2
PIECE = 5
NEAR = NZ * NX
BLK = NEAR * PIECE
FAR = NY * NC
STEP = 56
F32 = jnp.float32
BF16 = jnp.bfloat16


def feature_order():
    f = np.arange(D).reshape(NY, NZ, NX, NC, PIECE)
    return f.transpose(0, 3, 1, 2, 4).reshape(D).astype(np.int32)


def half_order():
    f = np.arange(D).reshape(NY, NZ, NX, NC, PIECE)[:, :, :, 0]
    return f.transpose(2, 0, 1, 3).reshape(D // NC).astype(np.int32)


def row_pick(places, near, padded):
    src = (np.arange(near)[None, :, None] * padded + places[:, None, :]).reshape(-1)
    return jnp.asarray(src[:, None] == np.arange(near * padded)[None, :], BF16)


def padded_rows(parts):
    rows = jnp.concatenate(parts, axis=0)
    return jnp.pad(rows, ((0, -rows.shape[0] % 8), (0, 0)))


def from_all(array, axis):
    copies = jnp.broadcast_to(array, (lax.axis_size(axis), *array.shape))
    return lax.all_to_all(copies, axis, split_axis=0, concat_axis=0, tiled=True)


def in_hbm(array):
    return pltpu.with_memory_space_constraint(array, pltpu.HBM)


def in_vmem(array):
    return pltpu.with_memory_space_constraint(array, pltpu.VMEM)


def dot(a, b):
    return jnp.dot(a, b, preferred_element_type=F32)


def dot_t(a, b):
    return lax.dot_general(a, b, (((1,), (1,)), ((), ())), preferred_element_type=F32)


def attention_body(
    x_ref, scale_ref, valid_ref, pool_ref, k_ref, vals_hbm, w_hbm, out_ref,
    w_buf, v_buf, q_buf, kn_buf, vn_buf, ctx_buf, sems,
):
    rows, width = q_buf.shape
    ctx_len = k_ref.shape[1]
    loads = [
        pltpu.make_async_copy(w_hbm.at[:, pl.ds(b * BLK, BLK), :], w_buf.at[b], sems.at[b])
        for b in range(4)
    ]
    load_v = pltpu.make_async_copy(vals_hbm, v_buf, sems.at[4])
    for load in loads[:3]:
        load.start()
    load_v.start()
    loads[3].start()
    x = x_ref[...]
    loads[0].wait()
    q = dot(x, w_buf[0].reshape(D, width))
    q_buf[...] = (q * scale_ref[...] / math.sqrt(HD)).astype(BF16).astype(F32)
    loads[1].wait()
    kn_buf[...] = dot(x, w_buf[1].reshape(D, width)).astype(BF16).astype(F32)
    loads[2].wait()
    vn_buf[...] = dot(x, w_buf[2].reshape(D, width)).astype(BF16).astype(F32)
    load_v.wait()
    pool = pool_ref[...]
    step = STEP

    def head_sums(prod):
        high = prod.astype(BF16)
        low = (prod - high.astype(F32)).astype(BF16)
        return dot(high, pool) + dot(low, pool)

    def body(i, carry):
        at = pl.multiple_of(i * step, 8)
        q8 = q_buf[pl.ds(at, step), :]
        k8 = k_ref[pl.ds(at, step)].astype(F32)
        prod = (q8[:, None, :] * k8).reshape(step * ctx_len, width)
        scores = head_sums(prod).reshape(step, ctx_len, 128)
        own = head_sums(q8 * kn_buf[pl.ds(at, step), :])
        used = valid_ref[pl.ds(at, step), :][:, None, :]
        slot = lax.broadcasted_iota(jnp.int32, (step, ctx_len, 128), 1)
        scores = jnp.where(slot < used, scores, -jnp.inf)
        top = jnp.maximum(jnp.max(scores, axis=1), own)
        e_cache = jnp.exp(scores - top[:, None, :])
        e_own = jnp.exp(own - top)
        total = jnp.sum(e_cache, axis=1) + e_own
        w_cache = (e_cache / total[:, None, :]).astype(BF16).reshape(step * ctx_len, 128)
        w_own = (e_own / total).astype(BF16)
        wide = dot_t(w_cache, pool).reshape(step, ctx_len, width)
        v8 = v_buf[pl.ds(at, step)].astype(F32)
        ctx = jnp.sum(wide * v8, axis=1)
        ctx_buf[pl.ds(at, step), :] = ctx + dot_t(w_own, pool) * vn_buf[pl.ds(at, step), :]
        return carry

    lax.fori_loop(0, rows // step, body, 0)
    loads[3].wait()
    out_ref[...] = dot_t(ctx_buf[...].astype(BF16), w_buf[3].reshape(D, width)).astype(BF16)


def attention_kernel(x, scale, valid, pool, keys, vals, w):
    rows, ctx_len, width = keys.shape
    vmem = pl.BlockSpec(memory_space=pltpu.VMEM)
    hbm = pl.BlockSpec(memory_space=pltpu.HBM)
    return pl.pallas_call(
        attention_body,
        out_shape=pltpu.VMEM((rows, D), BF16),
        in_specs=[vmem, vmem, vmem, vmem, vmem, hbm, hbm],
        out_specs=vmem,
        scratch_shapes=[
            pltpu.VMEM((4, FAR, BLK, width), BF16),
            pltpu.VMEM((rows, ctx_len, width), BF16),
            pltpu.VMEM((rows, width), F32),
            pltpu.VMEM((rows, width), F32),
            pltpu.VMEM((rows, width), F32),
            pltpu.VMEM((rows, width), F32),
            pltpu.SemaphoreType.DMA((5,)),
        ],
        compiler_params=pltpu.CompilerParams(vmem_limit_bytes=48 * 2**20),
        name="attend",
    )(x, scale, valid, pool, in_vmem(keys), in_hbm(vals), in_hbm(w))


def mlp_body(stream_ref, own_ref, other_ref, gain_ref, w_hbm, out_ref, w_buf, sems):
    loads = [
        pltpu.make_async_copy(w_hbm.at[:, pl.ds((4 + b) * BLK, BLK), :], w_buf.at[b], sems.at[b])
        for b in range(2)
    ]
    for load in loads:
        load.start()
    width = w_buf.shape[-1]
    s1 = stream_ref[...].astype(F32) + (own_ref[...].astype(F32) + other_ref[...].astype(F32))
    meansq = jnp.mean(s1 * s1, axis=-1, keepdims=True)
    n2 = (s1 * lax.rsqrt(meansq + 1e-06) * gain_ref[...]).astype(BF16)
    loads[0].wait()
    hidden = jnp.maximum(dot(n2, w_buf[0].reshape(D, width)), 0.0).astype(BF16)
    loads[1].wait()
    out_ref[...] = dot_t(hidden, w_buf[1].reshape(D, width)).astype(BF16)


def mlp_kernel(stream, own, other, gain, w):
    rows = stream.shape[0]
    vmem = pl.BlockSpec(memory_space=pltpu.VMEM)
    hbm = pl.BlockSpec(memory_space=pltpu.HBM)
    return pl.pallas_call(
        mlp_body,
        out_shape=pltpu.VMEM((rows, D), BF16),
        in_specs=[vmem, vmem, vmem, vmem, hbm],
        out_specs=vmem,
        scratch_shapes=[
            pltpu.VMEM((2, FAR, BLK, w.shape[-1]), BF16),
            pltpu.SemaphoreType.DMA((2,)),
        ],
        compiler_params=pltpu.CompilerParams(vmem_limit_bytes=32 * 2**20),
        name="mlp",
    )(stream, own, other, gain, in_hbm(w))


def head_body(
    stream_ref, own1_ref, other1_ref, own2_ref, other2_ref, far_ref, turn_hbm, back_hbm, near_hbm,
    mine_ref, give_ref, turn_buf, back_buf, w_buf, sems,
):
    width = w_buf.shape[-1]
    half = D // NC
    each = half // NX

    def rows(b):
        return pl.ds(b * each, each)

    def far(b):
        return far_ref[:, rows(b), :].reshape(half, width)

    def near(b):
        return w_buf[b].reshape(half, width)

    load_turn = pltpu.make_async_copy(turn_hbm, turn_buf, sems.at[0])
    load_back = pltpu.make_async_copy(back_hbm, back_buf, sems.at[1])
    loads = [
        pltpu.make_async_copy(near_hbm.at[:, rows(b), :], w_buf.at[b], sems.at[2 + b])
        for b in range(3)
    ]
    load_turn.start()
    loads[0].start()
    load_back.start()
    loads[1].start()
    loads[2].start()
    s1 = stream_ref[...].astype(F32) + (own1_ref[...].astype(F32) + other1_ref[...].astype(F32))
    s2 = (s1 + (own2_ref[...].astype(F32) + other2_ref[...].astype(F32))).astype(BF16)
    load_turn.wait()
    s2 = dot(s2, turn_buf[...]).astype(BF16)
    loads[0].wait()
    pre = dot(s2[:, :half], near(0)) + dot(s2[:, half:], far(0))
    act = (pre / (1.0 + jnp.exp(-pre))).astype(BF16)
    load_back.wait()
    s2_half = dot(s2, back_buf[:, :width]).astype(BF16)
    loads[1].wait()
    loads[2].wait()
    out = [dot_t(act, w(1)) + dot_t(s2_half, w(2)) for w in (near, far)]
    out = jnp.concatenate(out, axis=1).astype(BF16)
    give_ref[...] = dot(out, back_buf[:, width:]).astype(BF16)
    mine_ref[...] = dot(out, back_buf[:, :width]).astype(BF16)


def head_kernel(stream, own1, other1, own2, other2, turn, back, near, far):
    rows = stream.shape[0]
    width = near.shape[-1]
    vmem = pl.BlockSpec(memory_space=pltpu.VMEM)
    hbm = pl.BlockSpec(memory_space=pltpu.HBM)
    half = pltpu.VMEM((rows, width), BF16)
    return pl.pallas_call(
        head_body,
        out_shape=(half, half),
        in_specs=[vmem, vmem, vmem, vmem, vmem, vmem, hbm, hbm, hbm],
        out_specs=(vmem, vmem),
        scratch_shapes=[
            pltpu.VMEM((D, D), BF16),
            pltpu.VMEM((D, D), BF16),
            pltpu.VMEM((3, NX, D // NC // NX, width), BF16),
            pltpu.SemaphoreType.DMA((5,)),
        ],
        compiler_params=pltpu.CompilerParams(vmem_limit_bytes=32 * 2**20),
        name="head",
    )(stream, own1, other1, own2, other2, in_vmem(far), in_hbm(turn), in_hbm(back), in_hbm(near))


def rms_scale(values, gain):
    meansq = jnp.mean(values * values, axis=-1, keepdims=True)
    return values * lax.rsqrt(meansq + 1e-06) * gain


def swap(array):
    return lax.ppermute(array, "mp", [(0, 1), (1, 0)])


def per_device(
    new_embed,
    context_key_cache,
    value_cache,
    valid,
    attn_gain,
    mlp_gain,
    query_scale,
    w_qkv,
    w_out,
    w_up,
    w_down,
    head_hidden,
    final_layer_matrices,
):
    rows, _, width = context_key_cache.shape
    heads = width // HD
    piece = np.arange(PIECE)
    first = padded_rows(
        [jnp.transpose(w_qkv, (1, 0, 2)).reshape(3 * PIECE, width), w_out.T, w_up, w_down.T]
    )
    places = np.stack([piece * 3 + b for b in range(3)] + [piece + PIECE * b for b in range(3, 6)])
    shared = from_all(first, ("zh", "x")).reshape(-1, width)
    block1 = dot(row_pick(places, NEAR, first.shape[0]), shared).astype(BF16)
    block1, head_hidden, final_layer_matrices = lax.optimization_barrier(
        (block1, head_hidden, final_layer_matrices)
    )
    all1 = lax.all_gather(block1, ("y", "c"), axis=0)
    second = padded_rows(
        [head_hidden, jnp.transpose(final_layer_matrices, (0, 2, 1)).reshape(2 * PIECE, width)]
    )
    shared = from_all(second, "zh").reshape(-1, width)
    shared, new_embed = lax.optimization_barrier((shared, new_embed))
    shared = from_all(shared, "y").reshape(-1, width)
    places = np.stack([piece + PIECE * b for b in range(3)])
    block2 = dot(row_pick(places, NY * NZ, second.shape[0]), shared).astype(BF16)

    core = lax.axis_index("c")
    order = jnp.asarray(feature_order())
    half = jnp.asarray(half_order())
    order2 = jnp.concatenate([half + PIECE * core, half + PIECE * (1 - core)])
    ids = jnp.arange(D, dtype=jnp.int32)
    at = (ids + lax.axis_index("mp") * width) % D
    forth = (ids[:, None] == order[None, :]).astype(BF16)
    turn = (order[:, None] == order2[None, :]).astype(BF16)
    back = (order2[:, None] == at[None, :]).astype(BF16)

    normed = rms_scale(new_embed.astype(F32), attn_gain).astype(BF16)
    both = dot(jnp.concatenate([normed, new_embed], axis=0), forth).astype(BF16)
    normed_o, stream_o = both[:rows], both[rows:]
    gain_o = mlp_gain.reshape(NY, NZ, NX, NC, PIECE).transpose(0, 3, 1, 2, 4).reshape(1, D)
    pool = (jnp.arange(width)[:, None] // HD == jnp.arange(128)[None, :]).astype(BF16)
    scale = jnp.tile(query_scale, heads).reshape(1, width)
    used = jnp.broadcast_to(valid[:, None], (rows, 128))
    normed_o, stream_o, gain_o, pool, scale, used, turn, back, block2 = lax.optimization_barrier(
        (normed_o, stream_o, gain_o, pool, scale, used, turn, back, block2)
    )
    near = from_all(block2, "x")
    far = lax.ppermute(near, "c", [(0, 1), (1, 0)])

    part1 = attention_kernel(
        normed_o, scale, used, pool, context_key_cache, value_cache, all1
    )
    other1 = swap(part1)
    part2 = mlp_kernel(stream_o, part1, other1, gain_o, all1)
    mine, give = head_kernel(
        stream_o, part1, other1, part2, swap(part2), turn, back, near, far
    )
    return mine.astype(F32) + swap(give).astype(F32)


def solution(mesh):
    split = Mesh(
        mesh.devices.reshape(NY, NZ, NX, NC, mesh.shape["mp"]), ("y", "zh", "x", "c", "mp")
    )

    return jax.shard_map(
        per_device,
        mesh=split,
        in_specs=(
            P(DP, None),
            P(DP, None, "mp"),
            P(DP, None, "mp"),
            P(DP),
            P(),
            P(),
            P(),
            P(None, DP, "mp"),
            P("mp", DP),
            P(DP, "mp"),
            P("mp", DP),
            P(DP, "mp"),
            P(None, "mp", DP),
        ),
        out_specs=P(DP, "mp"),
        check_vma=False,
    )
```

profile of v0, /device:TPU:1, one launch (start us, length us, event | category | flops | bytes accessed | tf_op | source)
XLA Modules:
  0.0 182.4 jit_solution(17320677791497886448)
XLA Ops:
  6.5 0.0 copy-start.10
  6.5 0.0 copy-start.7
  6.5 0.0 all-gather.3.cloned.1.call-start
  6.5 0.8 reshape.69
  7.3 0.8 fusion.18
  8.1 0.0 copy-start.8
  8.1 0.0 copy-start.6
  8.1 0.1 broadcast_in_dim.10
  8.2 30.1 %all_to_all.20 = bf16[16,32,640]{2,1,0:T(8,128)(2,1)S(1)} all-to-all(bf16[16,32,640]{2,1,0:T(8,128)(2,1)S(1)} %broadcast_in_dim.10), channel_id=1, replica_groups=mesh['y'=8,'zh'=4,'x'=4,'c'=2,'mp'=2] {'zh','x'}, dimensions={0} | all-to-all | bytes 1310720 | tf_op jit(solution)/shard_map/all_to_all | solution.py:48
  38.2 2.4 %fusion.3 = bf16[480,640]{1,0:T(8,128)(2,1)} fusion(bf16[480,512]{1,0:T(8,128)(2,1)} %constant.51.clone, bf16[512,640]{1,0:T(8,128)(2,1)S(1)} %bitcast.20), kind=kOutput, calls=%fused_computation.8 | convolution fusion | flops 314880000 | bytes 1761280 | tf_op jit(solution)/shard_map/dot_general | solution.py:60
  40.6 0.0 all-gather.3.cloned.1.call-update
  40.7 0.0 copy-done.10
  40.7 0.1 reshape_tile.3.scale_ref
  40.8 0.0 copy-done.7
  40.8 0.3 reshape.73
  41.1 0.2 reshape.74.gain_ref
  41.3 0.0 copy-done.8
  41.4 0.0 copy-done.6
  41.4 0.0 copy-start.3
  41.4 0.0 copy-start.4
  41.4 3.4 %compare_convert_fusion = (bf16[1280,1280]{1,0:T(8,128)(2,1)}, bf16[1280,1280]{1,0:T(8,128)(2,1)}) fusion(s32[1280]{0:T(1024)S(1)} %get-tuple-element.43, s32[1280]{0:T(1024)S(1)} %get-tuple-element.44, s32[1280]{0:T(1024)S(1)} %copy-done.6), kind=kLoop, calls=%fused_computation.2 | loop fusion | flops 6553600 | bytes 6568960 | tf_op jit(solution)/shard_map/convert_element_type | solution.py:305
  44.8 0.0 copy-start.1
  44.8 0.0 copy-start.5
  44.8 0.0 copy-done.3
  44.8 0.0 copy-done.4
  44.9 0.6 broadcast_in_dim.11
  45.5 4.5 %all-to-all-start.1 = ((bf16[4,16,640]{2,1,0:T(8,128)(2,1)}), bf16[4,16,640]{2,1,0:T(8,128)(2,1)S(1)}, u32[]{:S(2)}, u32[]{:S(2)}) async-start(bf16[4,16,640]{2,1,0:T(8,128)(2,1)} %broadcast_in_dim.11), calls=%async_computation.1 | async-start | bytes 163840 | tf_op jit(solution)/shard_map/all_to_all | solution.py:48
  50.0 0.1 fusion.11.pool_ref
  50.2 6.8 %all-to-all-done.1 = bf16[4,16,640]{2,1,0:T(8,128)(2,1)S(1)} async-done(((bf16[4,16,640]{2,1,0:T(8,128)(2,1)}), bf16[4,16,640]{2,1,0:T(8,128)(2,1)S(1)}, u32[]{:S(2)}, u32[]{:S(2)}) %all-to-all-start.1) | async-done | bytes 81952 | tf_op jit(solution)/shard_map/all_to_all | solution.py:48
  57.0 0.9 broadcast_in_dim.13
  57.9 6.8 %all-to-all-start.2 = ((bf16[8,64,640]{2,1,0:T(8,128)(2,1)}), bf16[8,64,640]{2,1,0:T(8,128)(2,1)S(1)}, u32[]{:S(2)}, u32[]{:S(2)}) async-start(bf16[8,64,640]{2,1,0:T(8,128)(2,1)} %broadcast_in_dim.13), calls=%async_computation.2 | async-start | bytes 1310720 | tf_op jit(solution)/shard_map/all_to_all | solution.py:48
  64.8 0.0 copy-done.1
  64.8 0.1 fusion.5
  64.9 0.0 copy-done.5
  64.9 0.1 fusion.7
  65.1 0.0 copy-start.2
  65.1 1.5 fusion.2
  66.6 0.0 copy-start.9
  66.7 24.0 %all-to-all-done.2 = bf16[8,64,640]{2,1,0:T(8,128)(2,1)S(1)} async-done(((bf16[8,64,640]{2,1,0:T(8,128)(2,1)}), bf16[8,64,640]{2,1,0:T(8,128)(2,1)S(1)}, u32[]{:S(2)}, u32[]{:S(2)}) %all-to-all-start.2) | async-done | bytes 655392 | tf_op jit(solution)/shard_map/all_to_all | solution.py:48
  90.6 0.0 copy-done.2
  90.6 0.5 fusion.4
  91.2 0.0 copy-done.9
  91.2 0.1 broadcast_in_dim.12.valid_ref
  91.2 0.2 broadcast_in_dim.14
  91.5 29.0 %all_to_all.21.near_hbm = bf16[4,480,640]{2,1,0:T(8,128)(2,1)} all-to-all(bf16[4,480,640]{2,1,0:T(8,128)(2,1)S(1)} %broadcast_in_dim.14), channel_id=1, replica_groups=mesh['y'=8,'zh'=4,'x'=4,'c'=2,'mp'=2] {'x'}, dimensions={0} | all-to-all | bytes 4915200 | tf_op jit(solution)/shard_map/all_to_all | solution.py:48
  120.5 7.3 %collective-permute-start.2 = (bf16[4,480,640]{2,1,0:T(8,128)(2,1)}, bf16[4,480,640]{2,1,0:T(8,128)(2,1)S(1)}, u32[]{:S(2)}, u32[]{:S(2)}) collective-permute-start(bf16[4,480,640]{2,1,0:T(8,128)(2,1)} %all_to_all.21.near_hbm), channel_id=1, source_target_pairs={{0,2},{2,0},{1,3},{3,1},{4,6},{6,4},{5,7},{7,5},{8,10},{10,8},{9,1... | collective-permute-start | bytes 7372808 | tf_op jit(solution)/shard_map/ppermute | solution.py:318
  127.8 0.0 all-gather.3.cloned.1.call-done
  127.8 0.0 copy-start
  127.8 1.6 copy-done
  129.4 7.0 %attend.1.own_ref.own1_ref = bf16[112,1280]{1,0:T(8,128)(2,1)S(1)} custom-call(bf16[112,1280]{1,0:T(8,128)(2,1)S(1)} %get-tuple-element.26.x_ref, f32[1,640]{1,0:T(1,128)S(1)} %reshape_tile.3.scale_ref, s32[112,128]{1,0:T(8,128)S(1)} %broadcast_in_dim.12.valid_ref, bf16[640,128]{1,0:T(8,128)(2,1)S(1)} %fusion.11.pool_ref, bf16[112,16,640]{2,1,0:T(8,128)(2,1)S(1)} %copy-done, ...), custom_call_target="tpu_custom_call" | custom-call | tf_op jit(solution)/shard_map/attend/pallas_call | solution.py:130
  136.5 7.3 %collective-permute-start = (bf16[112,1280]{1,0:T(8,128)(2,1)S(1)}, bf16[112,1280]{1,0:T(8,128)(2,1)S(1)}, u32[]{:S(2)}, u32[]{:S(2)}) collective-permute-start(bf16[112,1280]{1,0:T(8,128)(2,1)S(1)} %attend.1.own_ref.own1_ref), channel_id=1, source_target_pairs={{0,1},{1,0},{2,3},{3,2},{4,5},{5,4},{6,7},{7,6},{8,9},{9,8},{10,11... | collective-permute-start | bytes 860168 | tf_op jit(solution)/shard_map/ppermute | solution.py:257
  143.8 7.2 %collective-permute-done.other_ref.other1_ref = bf16[112,1280]{1,0:T(8,128)(2,1)S(1)} collective-permute-done((bf16[112,1280]{1,0:T(8,128)(2,1)S(1)}, bf16[112,1280]{1,0:T(8,128)(2,1)S(1)}, u32[]{:S(2)}, u32[]{:S(2)}) %collective-permute-start) | collective-permute-done | bytes 286752 | tf_op jit(solution)/shard_map/ppermute | solution.py:257
  150.9 2.7 %mlp.1.own2_ref = bf16[112,1280]{1,0:T(8,128)(2,1)S(1)} custom-call(bf16[112,1280]{1,0:T(8,128)(2,1)S(1)} %get-tuple-element.25.stream_ref, bf16[112,1280]{1,0:T(8,128)(2,1)S(1)} %attend.1.own_ref.own1_ref, bf16[112,1280]{1,0:T(8,128)(2,1)S(1)} %collective-permute-done.other_ref.other1_ref, f32[1,1280]{1,0:T(1,128)S(1)} %reshape.74.gain_ref, ...), custom_call_target="tpu_custom_call" | custom-call | tf_op jit(solution)/shard_map/mlp/pallas_call | solution.py:170
  153.6 3.3 %collective-permute-start.1 = (bf16[112,1280]{1,0:T(8,128)(2,1)S(1)}, bf16[112,1280]{1,0:T(8,128)(2,1)S(1)}, u32[]{:S(2)}, u32[]{:S(2)}) collective-permute-start(bf16[112,1280]{1,0:T(8,128)(2,1)S(1)} %mlp.1.own2_ref), channel_id=1, source_target_pairs={{0,1},{1,0},{2,3},{3,2},{4,5},{5,4},{6,7},{7,6},{8,9},{9,8},{10,11... | collective-permute-start | bytes 860168 | tf_op jit(solution)/shard_map/ppermute | solution.py:257
  156.9 0.0 collective-permute-done.2.far_ref
  156.9 6.4 %collective-permute-done.1.other2_ref = bf16[112,1280]{1,0:T(8,128)(2,1)S(1)} collective-permute-done((bf16[112,1280]{1,0:T(8,128)(2,1)S(1)}, bf16[112,1280]{1,0:T(8,128)(2,1)S(1)}, u32[]{:S(2)}, u32[]{:S(2)}) %collective-permute-start.1) | collective-permute-done | bytes 286752 | tf_op jit(solution)/shard_map/ppermute | solution.py:257
  163.3 5.6 %head.1 = (bf16[112,640]{1,0:T(8,128)(2,1)S(1)}, bf16[112,640]{1,0:T(8,128)(2,1)S(1)}) custom-call(bf16[112,1280]{1,0:T(8,128)(2,1)S(1)} %get-tuple-element.25.stream_ref, bf16[112,1280]{1,0:T(8,128)(2,1)S(1)} %attend.1.own_ref.own1_ref, bf16[112,1280]{1,0:T(8,128)(2,1)S(1)} %collective-permute-done.other_ref.other1_ref, bf16[112,1280]{1,0:T(8,128)(2,1)S(1)} %mlp.1.own2_ref, ...), custom_call_target="tpu_custom_call" | custom-call | tf_op jit(solution)/shard_map/head/pallas_call | solution.py:235
  169.0 2.8 %collective-permute-start.3 = (bf16[112,640]{1,0:T(8,128)(2,1)S(1)}, bf16[112,640]{1,0:T(8,128)(2,1)S(1)}, u32[]{:S(2)}, u32[]{:S(2)}) collective-permute-start(bf16[112,640]{1,0:T(8,128)(2,1)S(1)} %get-tuple-element.36), channel_id=1, source_target_pairs={{0,1},{1,0},{2,3},{3,2},{4,5},{5,4},{6,7},{7,6},{8,9},{9,8},{10,11... | collective-permute-start | bytes 430088 | tf_op jit(solution)/shard_map/ppermute | solution.py:257
  171.8 3.0 %collective-permute-done.3 = bf16[112,640]{1,0:T(8,128)(2,1)S(1)} collective-permute-done((bf16[112,640]{1,0:T(8,128)(2,1)S(1)}, bf16[112,640]{1,0:T(8,128)(2,1)S(1)}, u32[]{:S(2)}, u32[]{:S(2)}) %collective-permute-start.3) | collective-permute-done | bytes 143392 | tf_op jit(solution)/shard_map/ppermute | solution.py:257
  174.8 0.7 convert_add_fusion
  (10 shorter events, 0.2 us)
Async XLA Ops:
  6.5 34.1 %copy-start.10 = (f32[80]{0:T(128)S(1)}, f32[80]{0:T(128)}, u32[]{:S(2)}) copy-start(f32[80]{0:T(128)} %param.23) | copy-start | bytes 964
  6.5 34.2 %copy-start.7 = (f32[1280]{0:T(1024)S(1)}, f32[1280]{0:T(1024)}, u32[]{:S(2)}) copy-start(f32[1280]{0:T(1024)} %param.22) | copy-start | bytes 15364
  6.5 121.2 %all-gather.3.cloned.1.call-start = ((), (), s32[]{:S(2)}) async-start(), calls=%async_computation.4 | async-start | bytes 10444800 | tf_op jit(solution)/shard_map/all_gather | solution.py:287
  8.1 33.2 %copy-start.8 = (s32[640]{0:T(1024)S(1)}, s32[640]{0:T(1024)}, u32[]{:S(2)}) copy-start(s32[640]{0:T(1024)} %constant.54.clone) | copy-start | bytes 7684
  8.1 33.3 %copy-start.6 = (s32[1280]{0:T(1024)S(1)}, s32[1280]{0:T(1024)}, u32[]{:S(2)}) copy-start(s32[1280]{0:T(1024)} %constant.53.clone) | copy-start | bytes 15364
  41.4 3.4 %copy-start.3 = (bf16[2,640,5]{1,0,2:T(2,128)(2,1)S(1)}, bf16[2,640,5]{1,0,2:T(2,128)(2,1)}, u32[]{:S(2)}) copy-start(bf16[2,640,5]{1,0,2:T(2,128)(2,1)} %param.29) | copy-start | bytes 38404
  41.4 3.5 %copy-start.4 = (bf16[5,640]{1,0:T(8,128)(2,1)S(1)}, bf16[5,640]{1,0:T(8,128)(2,1)}, u32[]{:S(2)}) copy-start(bf16[5,640]{1,0:T(8,128)(2,1)} %param.28) | copy-start | bytes 19204
  44.8 20.0 %copy-start.1 = (bf16[112,1280]{1,0:T(8,128)(2,1)S(1)}, bf16[112,1280]{1,0:T(8,128)(2,1)}, u32[]{:S(2)}) copy-start(bf16[112,1280]{1,0:T(8,128)(2,1)} %param.17) | copy-start | bytes 860164
  44.8 20.1 %copy-start.5 = (f32[1280]{0:T(1024)S(1)}, f32[1280]{0:T(1024)}, u32[]{:S(2)}) copy-start(f32[1280]{0:T(1024)} %param.21) | copy-start | bytes 15364
  45.5 11.5 %all-to-all-start.1 = ((bf16[4,16,640]{2,1,0:T(8,128)(2,1)}), bf16[4,16,640]{2,1,0:T(8,128)(2,1)S(1)}, u32[]{:S(2)}, u32[]{:S(2)}) async-start(bf16[4,16,640]{2,1,0:T(8,128)(2,1)} %broadcast_in_dim.11), calls=%async_computation.1 | async-start | bytes 163840 | tf_op jit(solution)/shard_map/all_to_all | solution.py:48
  57.9 32.7 %all-to-all-start.2 = ((bf16[8,64,640]{2,1,0:T(8,128)(2,1)}), bf16[8,64,640]{2,1,0:T(8,128)(2,1)S(1)}, u32[]{:S(2)}, u32[]{:S(2)}) async-start(bf16[8,64,640]{2,1,0:T(8,128)(2,1)} %broadcast_in_dim.13), calls=%async_computation.2 | async-start | bytes 1310720 | tf_op jit(solution)/shard_map/all_to_all | solution.py:48
  65.1 25.5 %copy-start.2 = (bf16[480,512]{1,0:T(8,128)(2,1)S(1)}, bf16[480,512]{1,0:T(8,128)(2,1)}, u32[]{:S(2)}) copy-start(bf16[480,512]{1,0:T(8,128)(2,1)} %constant.52.clone) | copy-start | bytes 1474564
  66.6 24.6 %copy-start.9 = (s32[112]{0:T(128)S(1)}, s32[112]{0:T(128)}, u32[]{:S(2)}) copy-start(s32[112]{0:T(128)} %param.20) | copy-start | bytes 1348
  120.5 36.5 %collective-permute-start.2 = (bf16[4,480,640]{2,1,0:T(8,128)(2,1)}, bf16[4,480,640]{2,1,0:T(8,128)(2,1)S(1)}, u32[]{:S(2)}, u32[]{:S(2)}) collective-permute-start(bf16[4,480,640]{2,1,0:T(8,128)(2,1)} %all_to_all.21.near_hbm), channel_id=1, source_target_pairs={{0,2},{2,0},{1,3},{3,1},{4,6},{6,4},{5,7},{7,5},{8,10},{10,8},{9,1... | collective-permute-start | bytes 7372808 | tf_op jit(solution)/shard_map/ppermute | solution.py:318
  127.8 1.6 copy-start
  136.5 14.4 %collective-permute-start = (bf16[112,1280]{1,0:T(8,128)(2,1)S(1)}, bf16[112,1280]{1,0:T(8,128)(2,1)S(1)}, u32[]{:S(2)}, u32[]{:S(2)}) collective-permute-start(bf16[112,1280]{1,0:T(8,128)(2,1)S(1)} %attend.1.own_ref.own1_ref), channel_id=1, source_target_pairs={{0,1},{1,0},{2,3},{3,2},{4,5},{5,4},{6,7},{7,6},{8,9},{9,8},{10,11... | collective-permute-start | bytes 860168 | tf_op jit(solution)/shard_map/ppermute | solution.py:257
  153.6 9.7 %collective-permute-start.1 = (bf16[112,1280]{1,0:T(8,128)(2,1)S(1)}, bf16[112,1280]{1,0:T(8,128)(2,1)S(1)}, u32[]{:S(2)}, u32[]{:S(2)}) collective-permute-start(bf16[112,1280]{1,0:T(8,128)(2,1)S(1)} %mlp.1.own2_ref), channel_id=1, source_target_pairs={{0,1},{1,0},{2,3},{3,2},{4,5},{5,4},{6,7},{7,6},{8,9},{9,8},{10,11... | collective-permute-start | bytes 860168 | tf_op jit(solution)/shard_map/ppermute | solution.py:257
  169.0 5.8 %collective-permute-start.3 = (bf16[112,640]{1,0:T(8,128)(2,1)S(1)}, bf16[112,640]{1,0:T(8,128)(2,1)S(1)}, u32[]{:S(2)}, u32[]{:S(2)}) collective-permute-start(bf16[112,640]{1,0:T(8,128)(2,1)S(1)} %get-tuple-element.36), channel_id=1, source_target_pairs={{0,1},{1,0},{2,3},{3,2},{4,5},{5,4},{6,7},{7,6},{8,9},{9,8},{10,11... | collective-permute-start | bytes 430088 | tf_op jit(solution)/shard_map/ppermute | solution.py:257
Sparse Core Ops, SparseCore 0:
  40.8 79.7 all-gather.2
where the time goes:
time: 183 us; the launch traced here: 182 us
  blocking collectives  59.1 us (32%)
  waiting for transfers between devices  47.4 us (26%)
  starting transfers between devices  32 us (17%)
  Pallas kernels  15.4 us (8%)
  between operations  13.7 us (7%)
  other arithmetic  5.39 us (3%)
  local copies, waits for them, and re-layouts  5.01 us (3%)
  matrix products  4.46 us (2%)
    all_to_all x2, blocking collectives, from_all(): return lax.all_to_all(copies, axis, split_axis=0, concat_axis=0, tiled=True)  59.1 us
    all_to_all x2, waiting for transfers between devices, from_all(): return lax.all_to_all(copies, axis, split_axis=0, concat_axis=0, tiled=True)  30.8 us
    ppermute x3, waiting for transfers between devices, swap(): return lax.ppermute(array, 'mp', [(0, 1), (1, 0)])  16.6 us
    ppermute x3, starting transfers between devices, swap(): return lax.ppermute(array, 'mp', [(0, 1), (1, 0)])  13.3 us
    all_to_all x2, starting transfers between devices, from_all(): return lax.all_to_all(copies, axis, split_axis=0, concat_axis=0, tiled=True)  11.3 us
    ppermute x1, starting transfers between devices, per_device(): far = lax.ppermute(near, 'c', [(0, 1), (1, 0)])  7.3 us
    pallas_call x1, Pallas kernels, attention_kernel(): pl.pallas_call(attention_body, out_shape=pltpu.VMEM((rows, D), BF16), in_...  7.04 us
    pallas_call x1, Pallas kernels, head_kernel(): pl.pallas_call(head_body, out_shape=(half, half), in_specs=[vmem, vmem, v...  5.64 us
  transfers between devices with their start and end apart: 7, of which 5 were waited for; matrix products, arithmetic and copies ran while one was open for 5% of the time, Pallas kernels for 5%

commit v1 on v0

--- a/solution.py
+++ b/solution.py
@@ -30,12 +30,37 @@
 
 def half_order():
     f = np.arange(D).reshape(NY, NZ, NX, NC, PIECE)[:, :, :, 0]
-    return f.transpose(2, 0, 1, 3).reshape(D // NC).astype(np.int32)
+    return f.transpose(2, 1, 0, 3).reshape(D // NC).astype(np.int32)
+
+
+def output_order():
+    f = np.arange(D // 2).reshape(NY // 2, NZ, NX, NC, PIECE)[:, :, :, 0]
+    return f.transpose(2, 1, 0, 3).reshape(D // 2 // NC).astype(np.int32)
+
+
+def output_rows(padded):
+    zh, y, piece = np.meshgrid(np.arange(NZ), np.arange(NY), np.arange(PIECE), indexing="ij")
+
+    def at(slot, row):
+        return (zh * NY + slot) * padded + row + piece
+
+    def halves(row):
+        src = at(y, row)
+        return np.concatenate([src[:, : NY // 2].reshape(-1), src[:, NY // 2 :].reshape(-1)])
+
+    own = at(y, 0).reshape(-1)
+    other = at((y + NY // 2) % NY, PIECE).reshape(-1)
+    return np.concatenate([own, other, halves(2 * PIECE), halves(3 * PIECE)])
 
 
 def row_pick(places, near, padded):
     src = (np.arange(near)[None, :, None] * padded + places[:, None, :]).reshape(-1)
-    return jnp.asarray(src[:, None] == np.arange(near * padded)[None, :], BF16)
+    return one_hot(src, near * padded)
+
+
+def one_hot(src, count):
+    src = jnp.asarray(src.astype(np.int32))
+    return (src[:, None] == jnp.arange(count, dtype=jnp.int32)[None, :]).astype(BF16)
 
 
 def padded_rows(parts):
@@ -182,70 +207,87 @@
 
 
 def head_body(
-    stream_ref, own1_ref, other1_ref, own2_ref, other2_ref, far_ref, turn_hbm, back_hbm, near_hbm,
-    mine_ref, give_ref, turn_buf, back_buf, w_buf, sems,
+    stream_ref, own1_ref, other1_ref, own2_ref, other2_ref, first_ref, far_ref,
+    turn_hbm, plain_hbm, last_hbm, near_hbm,
+    out_ref, turn_buf, plain_buf, last_buf, near_ref, sems,
 ):
-    width = w_buf.shape[-1]
+    width = near_ref.shape[-1]
     half = D // NC
     each = half // NX
-
-    def rows(b):
-        return pl.ds(b * each, each)
-
-    def far(b):
-        return far_ref[:, rows(b), :].reshape(half, width)
-
-    def near(b):
-        return w_buf[b].reshape(half, width)
-
-    load_turn = pltpu.make_async_copy(turn_hbm, turn_buf, sems.at[0])
-    load_back = pltpu.make_async_copy(back_hbm, back_buf, sems.at[1])
-    loads = [
-        pltpu.make_async_copy(near_hbm.at[:, rows(b), :], w_buf.at[b], sems.at[2 + b])
-        for b in range(3)
+    copies = [
+        pltpu.make_async_copy(src, dst, sems.at[n])
+        for n, (src, dst) in enumerate(
+            (
+                (turn_hbm, turn_buf),
+                (near_hbm, near_ref),
+                (plain_hbm, plain_buf),
+                (last_hbm, last_buf),
+            )
+        )
     ]
-    load_turn.start()
-    loads[0].start()
-    load_back.start()
-    loads[1].start()
-    loads[2].start()
+    for copy in copies:
+        copy.start()
+
+    def part(ref, start, count):
+        return ref[:, pl.ds(start, count), :].reshape(NX * count, width)
+
     s1 = stream_ref[...].astype(F32) + (own1_ref[...].astype(F32) + other1_ref[...].astype(F32))
     s2 = (s1 + (own2_ref[...].astype(F32) + other2_ref[...].astype(F32))).astype(BF16)
-    load_turn.wait()
-    s2 = dot(s2, turn_buf[...]).astype(BF16)
-    loads[0].wait()
-    pre = dot(s2[:, :half], near(0)) + dot(s2[:, half:], far(0))
-    act = (pre / (1.0 + jnp.exp(-pre))).astype(BF16)
-    load_back.wait()
-    s2_half = dot(s2, back_buf[:, :width]).astype(BF16)
-    loads[1].wait()
-    loads[2].wait()
-    out = [dot_t(act, w(1)) + dot_t(s2_half, w(2)) for w in (near, far)]
-    out = jnp.concatenate(out, axis=1).astype(BF16)
-    give_ref[...] = dot(out, back_buf[:, width:]).astype(BF16)
-    mine_ref[...] = dot(out, back_buf[:, :width]).astype(BF16)
-
-
-def head_kernel(stream, own1, other1, own2, other2, turn, back, near, far):
+    copies[0].wait()
+    turned = dot(s2, turn_buf[...]).astype(BF16)
+    copies[1].wait()
+
+    def hidden(start):
+        pre = dot(turned[:, :half], part(near_ref, start, each))
+        pre = pre + dot(turned[:, half:], part(far_ref, start, each))
+        return (pre / (1.0 + jnp.exp(-pre))).astype(BF16)
+
+    act_own = hidden(0)
+    act_other = hidden(each)
+    first = first_ref[...] > 0
+    act = (jnp.where(first, act_own, act_other), jnp.where(first, act_other, act_own))
+    copies[2].wait()
+    plain = dot(s2, plain_buf[...]).astype(BF16)
+    skip = (plain[:, :width], plain[:, width:])
+    out = []
+    for ref in (near_ref, far_ref):
+        total = None
+        for k in range(2):
+            at = 2 * each + k * (each // 2)
+            term = dot_t(act[k], part(ref, at, each // 2))
+            term = term + dot_t(skip[k], part(ref, at + each, each // 2))
+            total = term if total is None else total + term
+        out.append(total)
+    out = jnp.concatenate(out, axis=1)
+    high = out.astype(BF16)
+    low = (out - high.astype(F32)).astype(BF16)
+    copies[3].wait()
+    out_ref[...] = dot(high, last_buf[...]) + dot(low, last_buf[...])
+
+
+def head_kernel(stream, own1, other1, own2, other2, first, turn, plain, last, near, far):
     rows = stream.shape[0]
     width = near.shape[-1]
     vmem = pl.BlockSpec(memory_space=pltpu.VMEM)
     hbm = pl.BlockSpec(memory_space=pltpu.HBM)
-    half = pltpu.VMEM((rows, width), BF16)
     return pl.pallas_call(
         head_body,
-        out_shape=(half, half),
-        in_specs=[vmem, vmem, vmem, vmem, vmem, vmem, hbm, hbm, hbm],
-        out_specs=(vmem, vmem),
+        out_shape=jax.ShapeDtypeStruct((rows, width), F32),
+        in_specs=[vmem] * 7 + [hbm] * 4,
+        out_specs=vmem,
         scratch_shapes=[
-            pltpu.VMEM((D, D), BF16),
-            pltpu.VMEM((D, D), BF16),
-            pltpu.VMEM((3, NX, D // NC // NX, width), BF16),
-            pltpu.SemaphoreType.DMA((5,)),
+            pltpu.VMEM(turn.shape, BF16),
+            pltpu.VMEM(plain.shape, BF16),
+            pltpu.VMEM(last.shape, BF16),
+            pltpu.VMEM(near.shape, BF16),
+            pltpu.SemaphoreType.DMA((4,)),
         ],
         compiler_params=pltpu.CompilerParams(vmem_limit_bytes=32 * 2**20),
         name="head",
-    )(stream, own1, other1, own2, other2, in_vmem(far), in_hbm(turn), in_hbm(back), in_hbm(near))
+    )(
+        stream, own1, other1, own2, other2, first, in_vmem(far),
+        in_hbm(turn), in_hbm(plain), in_hbm(last), in_hbm(near),
+    )
 
 
 def rms_scale(values, gain):
@@ -275,34 +317,40 @@
     rows, _, width = context_key_cache.shape
     heads = width // HD
     piece = np.arange(PIECE)
+    y, core, mp = (lax.axis_index(axis) for axis in ("y", "c", "mp"))
+    local = padded_rows(
+        [head_hidden, jnp.transpose(final_layer_matrices, (0, 2, 1)).reshape(2 * PIECE, width)]
+    )
+    pairs = [(2 * a + m, 2 * ((a + NY // 2) % NY) + 1 - m) for a in range(NY) for m in range(2)]
+    got = lax.ppermute(local, ("y", "mp"), pairs)
+    keep = (y < NY // 2) == (mp == 0)
+    finals = jnp.where(keep, local[PIECE : 3 * PIECE], got[PIECE : 3 * PIECE])
+    second = padded_rows([local[:PIECE], got[:PIECE], finals])
     first = padded_rows(
         [jnp.transpose(w_qkv, (1, 0, 2)).reshape(3 * PIECE, width), w_out.T, w_up, w_down.T]
     )
     places = np.stack([piece * 3 + b for b in range(3)] + [piece + PIECE * b for b in range(3, 6)])
     shared = from_all(first, ("zh", "x")).reshape(-1, width)
+    shared2 = from_all(second, "y").reshape(-1, width)
     block1 = dot(row_pick(places, NEAR, first.shape[0]), shared).astype(BF16)
-    block1, head_hidden, final_layer_matrices = lax.optimization_barrier(
-        (block1, head_hidden, final_layer_matrices)
-    )
+    order = jnp.asarray(feature_order())
     all1 = lax.all_gather(block1, ("y", "c"), axis=0)
-    second = padded_rows(
-        [head_hidden, jnp.transpose(final_layer_matrices, (0, 2, 1)).reshape(2 * PIECE, width)]
-    )
-    shared = from_all(second, "zh").reshape(-1, width)
-    shared, new_embed = lax.optimization_barrier((shared, new_embed))
-    shared = from_all(shared, "y").reshape(-1, width)
-    places = np.stack([piece + PIECE * b for b in range(3)])
-    block2 = dot(row_pick(places, NY * NZ, second.shape[0]), shared).astype(BF16)
-
-    core = lax.axis_index("c")
-    order = jnp.asarray(feature_order())
+    _, shared2, new_embed, order = lax.optimization_barrier(
+        (block1, shared2, new_embed, order)
+    )
+    shared2 = from_all(shared2, "zh").reshape(-1, width)
+    pick = one_hot(output_rows(second.shape[0]), shared2.shape[0])
+    block2 = dot(pick, shared2).astype(BF16)
+
     half = jnp.asarray(half_order())
     order2 = jnp.concatenate([half + PIECE * core, half + PIECE * (1 - core)])
+    outs = jnp.asarray(output_order())
+    outs = jnp.concatenate([outs + PIECE * core, outs + PIECE * (1 - core)])
     ids = jnp.arange(D, dtype=jnp.int32)
-    at = (ids + lax.axis_index("mp") * width) % D
     forth = (ids[:, None] == order[None, :]).astype(BF16)
     turn = (order[:, None] == order2[None, :]).astype(BF16)
-    back = (order2[:, None] == at[None, :]).astype(BF16)
+    plain = (order[:, None] == ids[None, :]).astype(BF16)
+    last = (outs[:, None] == ids[None, : D // 2]).astype(BF16)
 
     normed = rms_scale(new_embed.astype(F32), attn_gain).astype(BF16)
     both = dot(jnp.concatenate([normed, new_embed], axis=0), forth).astype(BF16)
@@ -311,8 +359,11 @@
     pool = (jnp.arange(width)[:, None] // HD == jnp.arange(128)[None, :]).astype(BF16)
     scale = jnp.tile(query_scale, heads).reshape(1, width)
     used = jnp.broadcast_to(valid[:, None], (rows, 128))
-    normed_o, stream_o, gain_o, pool, scale, used, turn, back, block2 = lax.optimization_barrier(
-        (normed_o, stream_o, gain_o, pool, scale, used, turn, back, block2)
+    is_first = jnp.broadcast_to((mp == 0).astype(F32), (1, width))
+    normed_o, stream_o, gain_o, pool, scale, used, is_first, turn, plain, last, block2 = (
+        lax.optimization_barrier(
+            (normed_o, stream_o, gain_o, pool, scale, used, is_first, turn, plain, last, block2)
+        )
     )
     near = from_all(block2, "x")
     far = lax.ppermute(near, "c", [(0, 1), (1, 0)])
@@ -322,10 +373,10 @@
     )
     other1 = swap(part1)
     part2 = mlp_kernel(stream_o, part1, other1, gain_o, all1)
-    mine, give = head_kernel(
-        stream_o, part1, other1, part2, swap(part2), turn, back, near, far
-    )
-    return mine.astype(F32) + swap(give).astype(F32)
+    other2 = swap(part2)
+    return head_kernel(
+        stream_o, part1, other1, part2, other2, is_first, turn, plain, last, near, far
+    )
 
 
 def solution(mesh):

time: 183 us -> 196 us (1.071)
  starting transfers between devices: 32 us -> 58.7 us
  waiting for transfers between devices: 47.4 us -> 30.8 us
  blocking collectives: 59.1 us -> 56.6 us
  local copies, waits for them, and re-layouts: 5.01 us -> 7.07 us
    all_to_all x2, waiting for transfers between devices: 30.8 us -> 16.7 us  [from_all(): return lax.all_to_all(copies, axis, split_axis=0, concat_axis=0, tiled=True)]
    ppermute x0 -> x1, starting transfers between devices: none -> 12.8 us  [per_device(): got = lax.ppermute(local, ('y', 'mp'), pairs)]
    ppermute x1, starting transfers between devices: 7.3 us -> 18.6 us  [per_device(): far = lax.ppermute(near, 'c', [(0, 1), (1, 0)])]
    ppermute x3 -> x2, starting transfers between devices: 13.3 us -> 20.3 us  [swap(): return lax.ppermute(array, 'mp', [(0, 1), (1, 0)])]
    all_to_all x2, starting transfers between devices: 11.3 us -> 7.05 us  [from_all(): return lax.all_to_all(copies, axis, split_axis=0, concat_axis=0, tiled=True)]
    ppermute x3 -> x2, waiting for transfers between devices: 16.6 us -> 13.6 us  [swap(): return lax.ppermute(array, 'mp', [(0, 1), (1, 0)])]
    all_to_all x2, blocking collectives: 59.1 us -> 56.6 us  [from_all(): return lax.all_to_all(copies, axis, split_axis=0, concat_axis=0, tiled=True)]
    convert_element_type x1 -> x2, other arithmetic: 3.4 us -> 4.7 us  [the longest x1 3.58 us: per_device(): plain = (order[:, None] == ids[None, :]).astype(BF16)]
  transfers between devices with their start and end apart: 7 -> 7, of which waited for: 5 -> 5; matrix products, arithmetic and copies ran while one was open for 5% -> 6% of each run, Pallas kernels for 5% -> 5%
where the time goes in v1:
time: 196 us; the launch traced here: 195 us
  starting transfers between devices  58.7 us (30%)
  blocking collectives  56.6 us (29%)
  waiting for transfers between devices  30.8 us (16%)
  Pallas kernels  17.2 us (9%)
  between operations  13.8 us (7%)
  local copies, waits for them, and re-layouts  7.07 us (4%)
  other arithmetic  6.06 us (3%)
  matrix products  4.65 us (2%)
    all_to_all x2, blocking collectives, from_all(): return lax.all_to_all(copies, axis, split_axis=0, concat_axis=0, tiled=True)  56.6 us
    ppermute x2, starting transfers between devices, swap(): return lax.ppermute(array, 'mp', [(0, 1), (1, 0)])  20.3 us
    ppermute x1, starting transfers between devices, per_device(): far = lax.ppermute(near, 'c', [(0, 1), (1, 0)])  18.6 us
    all_to_all x2, waiting for transfers between devices, from_all(): return lax.all_to_all(copies, axis, split_axis=0, concat_axis=0, tiled=True)  16.7 us
    ppermute x2, waiting for transfers between devices, swap(): return lax.ppermute(array, 'mp', [(0, 1), (1, 0)])  13.6 us
    ppermute x1, starting transfers between devices, per_device(): got = lax.ppermute(local, ('y', 'mp'), pairs)  12.8 us
    pallas_call x1, Pallas kernels, head_kernel(): pl.pallas_call(head_body, out_shape=jax.ShapeDtypeStruct((rows, width), F...  7.46 us
    pallas_call x1, Pallas kernels, attention_kernel(): pl.pallas_call(attention_body, out_shape=pltpu.VMEM((rows, D), BF16), in_...  7.07 us
  transfers between devices with their start and end apart: 7, of which 5 were waited for; matrix products, arithmetic and copies ran while one was open for 6% of the time, Pallas kernels for 5%

profile of v1, /device:TPU:1, one launch (start us, length us, event | category | flops | bytes accessed | tf_op | source)
XLA Modules:
  0.0 194.9 jit_solution(17809538392469687484)
XLA Ops:
  6.5 0.0 copy-start.5
  6.5 0.0 all-gather.3.cloned.1.call-start
  6.5 0.0 copy-start.4
  6.5 0.8 reshape.62
  7.3 0.0 copy-start.10
  7.3 0.0 copy-start.9
  7.4 0.8 fusion.24
  8.1 0.0 copy-start.12
  8.1 0.0 copy-start.8
  8.2 0.1 broadcast_in_dim.12
  8.2 30.1 %all_to_all.20 = bf16[16,32,640]{2,1,0:T(8,128)(2,1)S(1)} all-to-all(bf16[16,32,640]{2,1,0:T(8,128)(2,1)S(1)} %broadcast_in_dim.12), channel_id=1, replica_groups=mesh['y'=8,'zh'=4,'x'=4,'c'=2,'mp'=2] {'zh','x'}, dimensions={0} | all-to-all | bytes 1310720 | tf_op jit(solution)/shard_map/all_to_all | solution.py:73
  38.3 2.1 %convolution_convert_fusion = bf16[480,640]{1,0:T(8,128)(2,1)} fusion(bf16[512,640]{1,0:T(8,128)(2,1)S(1)} %bitcast.15, s32[480]{0:T(512)} %constant.48.clone), kind=kOutput, calls=%fused_computation.11 | convolution fusion | flops 315125760 | bytes 1271680 | tf_op jit(solution)/shard_map/dot_general | solution.py:85
  40.4 0.0 all-gather.3.cloned.1.call-update
  40.4 0.0 copy-done.5
  40.4 0.0 copy-done.4
  40.5 12.8 %collective-permute-start = (bf16[16,640]{1,0:T(8,128)(2,1)S(1)}, bf16[16,640]{1,0:T(8,128)(2,1)S(1)}, u32[]{:S(2)}, u32[]{:S(2)}) collective-permute-start(bf16[16,640]{1,0:T(8,128)(2,1)S(1)} %fusion.29), channel_id=1, source_target_pairs={{0,257},{1,256},{64,321},{65,320},{128,385},{129,384},{192,449},{1... | collective-permute-start | bytes 61448 | tf_op jit(solution)/shard_map/ppermute | solution.py:325
  53.3 0.0 copy-done.10
  53.3 0.1 iota_add_fusion
  53.4 0.0 copy-done.9
  53.4 0.0 copy-done.12
  53.4 0.1 reshape_tile.3.scale_ref
  53.5 0.0 copy-done.8
  53.5 0.3 reshape.66
  53.8 0.2 reshape.67.gain_ref
  54.0 0.4 collective-permute-done
  54.5 0.7 broadcast_in_dim.13
  55.2 0.0 copy-start.3
  55.2 3.5 %all-to-all-start.1 = ((bf16[8,24,640]{2,1,0:T(8,128)(2,1)}), bf16[8,24,640]{2,1,0:T(8,128)(2,1)S(1)}, u32[]{:S(2)}, u32[]{:S(2)}) async-start(bf16[8,24,640]{2,1,0:T(8,128)(2,1)} %broadcast_in_dim.13), calls=%async_computation.1 | async-start | bytes 491520 | tf_op jit(solution)/shard_map/all_to_all | solution.py:73
  58.7 0.0 copy-start.6
  58.7 0.1 fusion.14.pool_ref
  58.9 0.0 copy-start.7
  58.9 1.1 compare_convert_fusion.1.last_hbm
  60.0 11.0 %all-to-all-done.1 = bf16[8,24,640]{2,1,0:T(8,128)(2,1)S(1)} async-done(((bf16[8,24,640]{2,1,0:T(8,128)(2,1)}), bf16[8,24,640]{2,1,0:T(8,128)(2,1)S(1)}, u32[]{:S(2)}, u32[]{:S(2)}) %all-to-all-start.1) | async-done | bytes 245792 | tf_op jit(solution)/shard_map/all_to_all | solution.py:73
  71.1 1.0 broadcast_in_dim.16
  72.1 3.5 %all-to-all-start.2 = ((bf16[4,192,640]{2,1,0:T(8,128)(2,1)}), bf16[4,192,640]{2,1,0:T(8,128)(2,1)S(1)}, u32[]{:S(2)}, u32[]{:S(2)}) async-start(bf16[4,192,640]{2,1,0:T(8,128)(2,1)} %broadcast_in_dim.16), calls=%async_computation.2 | async-start | bytes 1966080 | tf_op jit(solution)/shard_map/all_to_all | solution.py:73
  75.6 0.0 copy-done.3
  75.6 0.1 fusion.7
  75.8 0.0 copy-done.6
  75.8 0.1 fusion.9
  75.9 0.0 copy-done.7
  76.0 1.5 fusion.3
  77.5 0.9 fusion.34
  78.3 3.6 %fusion.1 = (bf16[1280,1280]{1,0:T(8,128)(2,1)}, bf16[1280,1280]{1,0:T(8,128)(2,1)}) fusion(s32[1280]{0:T(1024)S(1)} %copy-done.7, s32[1280]{0:T(1024)S(1)} %pad_add_fusion), kind=kLoop, calls=%fused_computation.3 | loop fusion | flops 6553600 | bytes 6563840 | tf_op jit(solution)/shard_map/convert_element_type | solution.py:352
  81.9 5.7 %all-to-all-done.2 = bf16[4,192,640]{2,1,0:T(8,128)(2,1)S(1)} async-done(((bf16[4,192,640]{2,1,0:T(8,128)(2,1)}), bf16[4,192,640]{2,1,0:T(8,128)(2,1)S(1)}, u32[]{:S(2)}, u32[]{:S(2)}) %all-to-all-start.2) | async-done | bytes 983072 | tf_op jit(solution)/shard_map/all_to_all | solution.py:73
  87.6 0.0 copy-done.13
  87.6 1.0 fusion.5
  88.7 0.0 copy-done.11
  88.7 0.1 broadcast_in_dim.14.valid_ref
  88.8 0.3 broadcast_in_dim.17
  89.0 26.6 %all_to_all.21.near_hbm = bf16[4,640,640]{2,1,0:T(8,128)(2,1)} all-to-all(bf16[4,640,640]{2,1,0:T(8,128)(2,1)S(1)} %broadcast_in_dim.17), channel_id=1, replica_groups=mesh['y'=8,'zh'=4,'x'=4,'c'=2,'mp'=2] {'x'}, dimensions={0} | all-to-all | bytes 6553600 | tf_op jit(solution)/shard_map/all_to_all | solution.py:73
  115.6 18.6 %collective-permute-start.3 = (bf16[4,640,640]{2,1,0:T(8,128)(2,1)}, bf16[4,640,640]{2,1,0:T(8,128)(2,1)S(1)}, u32[]{:S(2)}, u32[]{:S(2)}) collective-permute-start(bf16[4,640,640]{2,1,0:T(8,128)(2,1)} %all_to_all.21.near_hbm), channel_id=1, source_target_pairs={{0,2},{2,0},{1,3},{3,1},{4,6},{6,4},{5,7},{7,5},{8,10},{10,8},{9,1... | collective-permute-start | bytes 9830408 | tf_op jit(solution)/shard_map/ppermute | solution.py:369
  134.2 0.0 all-gather.3.cloned.1.call-done
  134.2 0.0 copy-start.1
  134.3 1.6 copy-done.1
  135.9 1.0 copy-done.2
  136.9 7.1 %attend.1.own_ref.own1_ref = bf16[112,1280]{1,0:T(8,128)(2,1)S(1)} custom-call(bf16[112,1280]{1,0:T(8,128)(2,1)S(1)} %copy-done.2, f32[1,640]{1,0:T(1,128)S(1)} %reshape_tile.3.scale_ref, s32[112,128]{1,0:T(8,128)S(1)} %broadcast_in_dim.14.valid_ref, bf16[640,128]{1,0:T(8,128)(2,1)S(1)} %fusion.14.pool_ref, bf16[112,16,640]{2,1,0:T(8,128)(2,1)S(1)} %copy-done.1, ...), custom_call_target="tpu_custom_call" | custom-call | tf_op jit(solution)/shard_map/attend/pallas_call | solution.py:155
  143.9 17.0 %collective-permute-start.1 = (bf16[112,1280]{1,0:T(8,128)(2,1)S(1)}, bf16[112,1280]{1,0:T(8,128)(2,1)S(1)}, u32[]{:S(2)}, u32[]{:S(2)}) collective-permute-start(bf16[112,1280]{1,0:T(8,128)(2,1)S(1)} %attend.1.own_ref.own1_ref), channel_id=1, source_target_pairs={{0,1},{1,0},{2,3},{3,2},{4,5},{5,4},{6,7},{7,6},{8,9},{9,8},{10,11... | collective-permute-start | bytes 860168 | tf_op jit(solution)/shard_map/ppermute | solution.py:299
  161.0 7.2 %collective-permute-done.1.other_ref.other1_ref = bf16[112,1280]{1,0:T(8,128)(2,1)S(1)} collective-permute-done((bf16[112,1280]{1,0:T(8,128)(2,1)S(1)}, bf16[112,1280]{1,0:T(8,128)(2,1)S(1)}, u32[]{:S(2)}, u32[]{:S(2)}) %collective-permute-start.1) | collective-permute-done | bytes 286752 | tf_op jit(solution)/shard_map/ppermute | solution.py:299
  168.1 0.0 copy-done
  168.2 2.7 %mlp.1.own2_ref = bf16[112,1280]{1,0:T(8,128)(2,1)S(1)} custom-call(bf16[112,1280]{1,0:T(8,128)(2,1)S(1)} %copy-done, bf16[112,1280]{1,0:T(8,128)(2,1)S(1)} %attend.1.own_ref.own1_ref, bf16[112,1280]{1,0:T(8,128)(2,1)S(1)} %collective-permute-done.1.other_ref.other1_ref, f32[1,1280]{1,0:T(1,128)S(1)} %reshape.67.gain_ref, bf16[16,480,640]{2,1,0:T(8,128)(2,1)} %bitcast.12), custom_call_target="tpu_custom_call" | custom-call | tf_op jit(solution)/shard_map/mlp/pallas_call | solution.py:195
  170.9 3.3 %collective-permute-start.2 = (bf16[112,1280]{1,0:T(8,128)(2,1)S(1)}, bf16[112,1280]{1,0:T(8,128)(2,1)S(1)}, u32[]{:S(2)}, u32[]{:S(2)}) collective-permute-start(bf16[112,1280]{1,0:T(8,128)(2,1)S(1)} %mlp.1.own2_ref), channel_id=1, source_target_pairs={{0,1},{1,0},{2,3},{3,2},{4,5},{5,4},{6,7},{7,6},{8,9},{9,8},{10,11... | collective-permute-start | bytes 860168 | tf_op jit(solution)/shard_map/ppermute | solution.py:299
  174.1 0.0 collective-permute-done.3.far_ref
  174.1 6.4 %collective-permute-done.2.other2_ref = bf16[112,1280]{1,0:T(8,128)(2,1)S(1)} collective-permute-done((bf16[112,1280]{1,0:T(8,128)(2,1)S(1)}, bf16[112,1280]{1,0:T(8,128)(2,1)S(1)}, u32[]{:S(2)}, u32[]{:S(2)}) %collective-permute-start.2) | collective-permute-done | bytes 286752 | tf_op jit(solution)/shard_map/ppermute | solution.py:299
  180.6 7.5 %head.1 = f32[112,640]{1,0:T(8,128)} custom-call(bf16[112,1280]{1,0:T(8,128)(2,1)S(1)} %copy-done, bf16[112,1280]{1,0:T(8,128)(2,1)S(1)} %attend.1.own_ref.own1_ref, bf16[112,1280]{1,0:T(8,128)(2,1)S(1)} %collective-permute-done.1.other_ref.other1_ref, bf16[112,1280]{1,0:T(8,128)(2,1)S(1)} %mlp.1.own2_ref, ...), custom_call_target="tpu_custom_call" | custom-call | tf_op jit(solution)/shard_map/head/pallas_call | solution.py:273
  (18 shorter events, 0.2 us)
Async XLA Ops:
  6.5 33.9 %copy-start.5 = (bf16[2,640,5]{1,0,2:T(2,128)(2,1)S(1)}, bf16[2,640,5]{1,0,2:T(2,128)(2,1)}, u32[]{:S(2)}) copy-start(bf16[2,640,5]{1,0,2:T(2,128)(2,1)} %param.30) | copy-start | bytes 38404
  6.5 127.7 %all-gather.3.cloned.1.call-start = ((), (), s32[]{:S(2)}) async-start(), calls=%async_computation.4 | async-start | bytes 10444800 | tf_op jit(solution)/shard_map/all_gather | solution.py:337
  6.5 33.9 %copy-start.4 = (bf16[5,640]{1,0:T(8,128)(2,1)S(1)}, bf16[5,640]{1,0:T(8,128)(2,1)}, u32[]{:S(2)}) copy-start(bf16[5,640]{1,0:T(8,128)(2,1)} %param.29) | copy-start | bytes 19204
  7.3 45.9 %copy-start.10 = (s32[320]{0:T(512)S(1)}, s32[320]{0:T(512)}, u32[]{:S(2)}) copy-start(s32[320]{0:T(512)} %constant.52.clone) | copy-start | bytes 3844
  7.3 46.0 %copy-start.9 = (s32[640]{0:T(1024)S(1)}, s32[640]{0:T(1024)}, u32[]{:S(2)}) copy-start(s32[640]{0:T(1024)} %constant.51.clone) | copy-start | bytes 7684
  8.1 45.3 %copy-start.12 = (f32[80]{0:T(128)S(1)}, f32[80]{0:T(128)}, u32[]{:S(2)}) copy-start(f32[80]{0:T(128)} %param.24) | copy-start | bytes 964
  8.1 45.4 %copy-start.8 = (f32[1280]{0:T(1024)S(1)}, f32[1280]{0:T(1024)}, u32[]{:S(2)}) copy-start(f32[1280]{0:T(1024)} %param.23) | copy-start | bytes 15364
  40.5 14.0 %collective-permute-start = (bf16[16,640]{1,0:T(8,128)(2,1)S(1)}, bf16[16,640]{1,0:T(8,128)(2,1)S(1)}, u32[]{:S(2)}, u32[]{:S(2)}) collective-permute-start(bf16[16,640]{1,0:T(8,128)(2,1)S(1)} %fusion.29), channel_id=1, source_target_pairs={{0,257},{1,256},{64,321},{65,320},{128,385},{129,384},{192,449},{1... | collective-permute-start | bytes 61448 | tf_op jit(solution)/shard_map/ppermute | solution.py:325
  55.2 20.5 %copy-start.3 = (bf16[112,1280]{1,0:T(8,128)(2,1)S(1)}, bf16[112,1280]{1,0:T(8,128)(2,1)}, u32[]{:S(2)}) copy-start(bf16[112,1280]{1,0:T(8,128)(2,1)} %param.18) | copy-start | bytes 860164
  55.2 15.9 %all-to-all-start.1 = ((bf16[8,24,640]{2,1,0:T(8,128)(2,1)}), bf16[8,24,640]{2,1,0:T(8,128)(2,1)S(1)}, u32[]{:S(2)}, u32[]{:S(2)}) async-start(bf16[8,24,640]{2,1,0:T(8,128)(2,1)} %broadcast_in_dim.13), calls=%async_computation.1 | async-start | bytes 491520 | tf_op jit(solution)/shard_map/all_to_all | solution.py:73
  58.7 17.1 %copy-start.6 = (f32[1280]{0:T(1024)S(1)}, f32[1280]{0:T(1024)}, u32[]{:S(2)}) copy-start(f32[1280]{0:T(1024)} %param.22) | copy-start | bytes 15364
  58.9 17.1 %copy-start.7 = (s32[1280]{0:T(1024)S(1)}, s32[1280]{0:T(1024)}, u32[]{:S(2)}) copy-start(s32[1280]{0:T(1024)} %constant.49.clone) | copy-start | bytes 15364
  72.1 15.5 %all-to-all-start.2 = ((bf16[4,192,640]{2,1,0:T(8,128)(2,1)}), bf16[4,192,640]{2,1,0:T(8,128)(2,1)S(1)}, u32[]{:S(2)}, u32[]{:S(2)}) async-start(bf16[4,192,640]{2,1,0:T(8,128)(2,1)} %broadcast_in_dim.16), calls=%async_computation.2 | async-start | bytes 1966080 | tf_op jit(solution)/shard_map/all_to_all | solution.py:73
  78.3 9.3 %copy-start.13 = (s32[640]{0:T(1024)S(1)}, s32[640]{0:T(1024)}, u32[]{:S(2)}) copy-start(s32[640]{0:T(1024)} %constant.50.clone) | copy-start | bytes 7684
  81.9 6.8 %copy-start.11 = (s32[112]{0:T(128)S(1)}, s32[112]{0:T(128)}, u32[]{:S(2)}) copy-start(s32[112]{0:T(128)} %param.21) | copy-start | bytes 1348
  115.6 58.5 %collective-permute-start.3 = (bf16[4,640,640]{2,1,0:T(8,128)(2,1)}, bf16[4,640,640]{2,1,0:T(8,128)(2,1)S(1)}, u32[]{:S(2)}, u32[]{:S(2)}) collective-permute-start(bf16[4,640,640]{2,1,0:T(8,128)(2,1)} %all_to_all.21.near_hbm), channel_id=1, source_target_pairs={{0,2},{2,0},{1,3},{3,1},{4,6},{6,4},{5,7},{7,5},{8,10},{10,8},{9,1... | collective-permute-start | bytes 9830408 | tf_op jit(solution)/shard_map/ppermute | solution.py:369
  134.2 1.6 copy-start.1
  135.9 1.0 copy-start.2
  136.9 31.3 %copy-start = (bf16[112,1280]{1,0:T(8,128)(2,1)S(1)}, bf16[112,1280]{1,0:T(8,128)(2,1)}, u32[]{:S(2)}) copy-start(bf16[112,1280]{1,0:T(8,128)(2,1)} %get-tuple-element.22.stream_ref) | copy-start | bytes 860164
  143.9 24.2 %collective-permute-start.1 = (bf16[112,1280]{1,0:T(8,128)(2,1)S(1)}, bf16[112,1280]{1,0:T(8,128)(2,1)S(1)}, u32[]{:S(2)}, u32[]{:S(2)}) collective-permute-start(bf16[112,1280]{1,0:T(8,128)(2,1)S(1)} %attend.1.own_ref.own1_ref), channel_id=1, source_target_pairs={{0,1},{1,0},{2,3},{3,2},{4,5},{5,4},{6,7},{7,6},{8,9},{9,8},{10,11... | collective-permute-start | bytes 860168 | tf_op jit(solution)/shard_map/ppermute | solution.py:299
  170.9 9.7 %collective-permute-start.2 = (bf16[112,1280]{1,0:T(8,128)(2,1)S(1)}, bf16[112,1280]{1,0:T(8,128)(2,1)S(1)}, u32[]{:S(2)}, u32[]{:S(2)}) collective-permute-start(bf16[112,1280]{1,0:T(8,128)(2,1)S(1)} %mlp.1.own2_ref), channel_id=1, source_target_pairs={{0,1},{1,0},{2,3},{3,2},{4,5},{5,4},{6,7},{7,6},{8,9},{9,8},{10,11... | collective-permute-start | bytes 860168 | tf_op jit(solution)/shard_map/ppermute | solution.py:299
Sparse Core Ops, SparseCore 0:
  40.5 71.0 all-gather.2

commit v2 on v1

--- a/solution.py
+++ b/solution.py
@@ -53,9 +53,10 @@
     return np.concatenate([own, other, halves(2 * PIECE), halves(3 * PIECE)])
 
 
-def row_pick(places, near, padded):
-    src = (np.arange(near)[None, :, None] * padded + places[:, None, :]).reshape(-1)
-    return one_hot(src, near * padded)
+def matrix_rows(places, padded):
+    zh, x = np.meshgrid(np.arange(NZ), np.arange(NX), indexing="ij")
+    device = (x * NZ + zh).reshape(-1)
+    return (device[None, :, None] * padded + places[:, None, :]).reshape(-1)
 
 
 def one_hot(src, count):
@@ -90,7 +91,7 @@
 
 
 def attention_body(
-    x_ref, scale_ref, valid_ref, pool_ref, k_ref, vals_hbm, w_hbm, out_ref,
+    x_ref, scale_ref, valid_ref, pool_ref, k_ref, vals_hbm, w_hbm, out_ref, next_ref,
     w_buf, v_buf, q_buf, kn_buf, vn_buf, ctx_buf, sems,
 ):
     rows, width = q_buf.shape
@@ -99,16 +100,25 @@
         pltpu.make_async_copy(w_hbm.at[:, pl.ds(b * BLK, BLK), :], w_buf.at[b], sems.at[b])
         for b in range(4)
     ]
-    load_v = pltpu.make_async_copy(vals_hbm, v_buf, sems.at[4])
-    for load in loads[:3]:
-        load.start()
-    load_v.start()
-    loads[3].start()
+    later = [
+        pltpu.make_async_copy(
+            w_hbm.at[:, pl.ds((4 + b) * BLK, BLK), :], next_ref.at[b], sems.at[4 + b]
+        )
+        for b in range(2)
+    ]
+    load_v = pltpu.make_async_copy(vals_hbm, v_buf, sems.at[6])
+    loads[0].start()
+    loads[1].start()
     x = x_ref[...]
     loads[0].wait()
+    loads[2].start()
+    load_v.start()
     q = dot(x, w_buf[0].reshape(D, width))
     q_buf[...] = (q * scale_ref[...] / math.sqrt(HD)).astype(BF16).astype(F32)
     loads[1].wait()
+    loads[3].start()
+    for load in later:
+        load.start()
     kn_buf[...] = dot(x, w_buf[1].reshape(D, width)).astype(BF16).astype(F32)
     loads[2].wait()
     vn_buf[...] = dot(x, w_buf[2].reshape(D, width)).astype(BF16).astype(F32)
@@ -146,6 +156,8 @@
     lax.fori_loop(0, rows // step, body, 0)
     loads[3].wait()
     out_ref[...] = dot_t(ctx_buf[...].astype(BF16), w_buf[3].reshape(D, width)).astype(BF16)
+    for load in later:
+        load.wait()
 
 
 def attention_kernel(x, scale, valid, pool, keys, vals, w):
@@ -154,9 +166,9 @@
     hbm = pl.BlockSpec(memory_space=pltpu.HBM)
     return pl.pallas_call(
         attention_body,
-        out_shape=pltpu.VMEM((rows, D), BF16),
-        in_specs=[vmem, vmem, vmem, vmem, vmem, hbm, hbm],
-        out_specs=vmem,
+        out_shape=(pltpu.VMEM((rows, D), BF16), pltpu.VMEM((2, FAR, BLK, width), BF16)),
+        in_specs=[vmem] * 5 + [hbm] * 2,
+        out_specs=(vmem, vmem),
         scratch_shapes=[
             pltpu.VMEM((4, FAR, BLK, width), BF16),
             pltpu.VMEM((rows, ctx_len, width), BF16),
@@ -164,46 +176,33 @@
             pltpu.VMEM((rows, width), F32),
             pltpu.VMEM((rows, width), F32),
             pltpu.VMEM((rows, width), F32),
-            pltpu.SemaphoreType.DMA((5,)),
+            pltpu.SemaphoreType.DMA((7,)),
         ],
-        compiler_params=pltpu.CompilerParams(vmem_limit_bytes=48 * 2**20),
+        compiler_params=pltpu.CompilerParams(vmem_limit_bytes=36 * 2**20),
         name="attend",
     )(x, scale, valid, pool, in_vmem(keys), in_hbm(vals), in_hbm(w))
 
 
-def mlp_body(stream_ref, own_ref, other_ref, gain_ref, w_hbm, out_ref, w_buf, sems):
-    loads = [
-        pltpu.make_async_copy(w_hbm.at[:, pl.ds((4 + b) * BLK, BLK), :], w_buf.at[b], sems.at[b])
-        for b in range(2)
-    ]
-    for load in loads:
-        load.start()
-    width = w_buf.shape[-1]
+def mlp_body(stream_ref, own_ref, other_ref, gain_ref, w_ref, out_ref):
+    width = w_ref.shape[-1]
     s1 = stream_ref[...].astype(F32) + (own_ref[...].astype(F32) + other_ref[...].astype(F32))
     meansq = jnp.mean(s1 * s1, axis=-1, keepdims=True)
     n2 = (s1 * lax.rsqrt(meansq + 1e-06) * gain_ref[...]).astype(BF16)
-    loads[0].wait()
-    hidden = jnp.maximum(dot(n2, w_buf[0].reshape(D, width)), 0.0).astype(BF16)
-    loads[1].wait()
-    out_ref[...] = dot_t(hidden, w_buf[1].reshape(D, width)).astype(BF16)
+    hidden = jnp.maximum(dot(n2, w_ref[0].reshape(D, width)), 0.0).astype(BF16)
+    out_ref[...] = dot_t(hidden, w_ref[1].reshape(D, width)).astype(BF16)
 
 
 def mlp_kernel(stream, own, other, gain, w):
     rows = stream.shape[0]
     vmem = pl.BlockSpec(memory_space=pltpu.VMEM)
-    hbm = pl.BlockSpec(memory_space=pltpu.HBM)
     return pl.pallas_call(
         mlp_body,
         out_shape=pltpu.VMEM((rows, D), BF16),
-        in_specs=[vmem, vmem, vmem, vmem, hbm],
+        in_specs=[vmem] * 5,
         out_specs=vmem,
-        scratch_shapes=[
-            pltpu.VMEM((2, FAR, BLK, w.shape[-1]), BF16),
-            pltpu.SemaphoreType.DMA((2,)),
-        ],
-        compiler_params=pltpu.CompilerParams(vmem_limit_bytes=32 * 2**20),
+        compiler_params=pltpu.CompilerParams(vmem_limit_bytes=12 * 2**20),
         name="mlp",
-    )(stream, own, other, gain, in_hbm(w))
+    )(stream, own, other, gain, in_vmem(w))
 
 
 def head_body(
@@ -214,28 +213,32 @@
     width = near_ref.shape[-1]
     half = D // NC
     each = half // NX
-    copies = [
-        pltpu.make_async_copy(src, dst, sems.at[n])
-        for n, (src, dst) in enumerate(
-            (
-                (turn_hbm, turn_buf),
-                (near_hbm, near_ref),
-                (plain_hbm, plain_buf),
-                (last_hbm, last_buf),
-            )
+    rows = 2 * each
+    load_turn = pltpu.make_async_copy(turn_hbm, turn_buf, sems.at[0])
+    load_plain = pltpu.make_async_copy(plain_hbm, plain_buf, sems.at[1])
+    load_last = pltpu.make_async_copy(last_hbm, last_buf, sems.at[2])
+    loads = [
+        pltpu.make_async_copy(
+            near_hbm.at[:, pl.ds(n * rows, rows), :],
+            near_ref.at[:, pl.ds(n * rows, rows), :],
+            sems.at[3 + n],
         )
+        for n in range(2)
     ]
-    for copy in copies:
-        copy.start()
+    load_turn.start()
+    loads[0].start()
 
     def part(ref, start, count):
         return ref[:, pl.ds(start, count), :].reshape(NX * count, width)
 
     s1 = stream_ref[...].astype(F32) + (own1_ref[...].astype(F32) + other1_ref[...].astype(F32))
     s2 = (s1 + (own2_ref[...].astype(F32) + other2_ref[...].astype(F32))).astype(BF16)
-    copies[0].wait()
+    load_turn.wait()
+    load_plain.start()
+    loads[1].start()
+    load_last.start()
     turned = dot(s2, turn_buf[...]).astype(BF16)
-    copies[1].wait()
+    loads[0].wait()
 
     def hidden(start):
         pre = dot(turned[:, :half], part(near_ref, start, each))
@@ -246,9 +249,10 @@
     act_other = hidden(each)
     first = first_ref[...] > 0
     act = (jnp.where(first, act_own, act_other), jnp.where(first, act_other, act_own))
-    copies[2].wait()
+    load_plain.wait()
     plain = dot(s2, plain_buf[...]).astype(BF16)
     skip = (plain[:, :width], plain[:, width:])
+    loads[1].wait()
     out = []
     for ref in (near_ref, far_ref):
         total = None
@@ -261,7 +265,7 @@
     out = jnp.concatenate(out, axis=1)
     high = out.astype(BF16)
     low = (out - high.astype(F32)).astype(BF16)
-    copies[3].wait()
+    load_last.wait()
     out_ref[...] = dot(high, last_buf[...]) + dot(low, last_buf[...])
 
 
@@ -280,7 +284,7 @@
             pltpu.VMEM(plain.shape, BF16),
             pltpu.VMEM(last.shape, BF16),
             pltpu.VMEM(near.shape, BF16),
-            pltpu.SemaphoreType.DMA((4,)),
+            pltpu.SemaphoreType.DMA((5,)),
         ],
         compiler_params=pltpu.CompilerParams(vmem_limit_bytes=32 * 2**20),
         name="head",
@@ -330,9 +334,11 @@
         [jnp.transpose(w_qkv, (1, 0, 2)).reshape(3 * PIECE, width), w_out.T, w_up, w_down.T]
     )
     places = np.stack([piece * 3 + b for b in range(3)] + [piece + PIECE * b for b in range(3, 6)])
-    shared = from_all(first, ("zh", "x")).reshape(-1, width)
+    shared = from_all(first, "zh").reshape(-1, width)
+    shared = from_all(shared, "x").reshape(-1, width)
     shared2 = from_all(second, "y").reshape(-1, width)
-    block1 = dot(row_pick(places, NEAR, first.shape[0]), shared).astype(BF16)
+    pick = one_hot(matrix_rows(places, first.shape[0]), shared.shape[0])
+    block1 = dot(pick, shared).astype(BF16)
     order = jnp.asarray(feature_order())
     all1 = lax.all_gather(block1, ("y", "c"), axis=0)
     _, shared2, new_embed, order = lax.optimization_barrier(
@@ -368,11 +374,11 @@
     near = from_all(block2, "x")
     far = lax.ppermute(near, "c", [(0, 1), (1, 0)])
 
-    part1 = attention_kernel(
+    part1, feed_w = attention_kernel(
         normed_o, scale, used, pool, context_key_cache, value_cache, all1
     )
     other1 = swap(part1)
-    part2 = mlp_kernel(stream_o, part1, other1, gain_o, all1)
+    part2 = mlp_kernel(stream_o, part1, other1, gain_o, feed_w)
     other2 = swap(part2)
     return head_kernel(
         stream_o, part1, other1, part2, other2, is_first, turn, plain, last, near, far

time: 196 us -> 192 us (0.980)
  starting transfers between devices: 58.7 us -> 45.7 us
  blocking collectives: 56.6 us -> 62.1 us
  waiting for transfers between devices: 30.8 us -> 36.2 us
    ppermute x2, starting transfers between devices: 20.3 us -> 12.3 us  [swap(): return lax.ppermute(array, 'mp', [(0, 1), (1, 0)])]
    ppermute x1, starting transfers between devices: 18.6 us -> 13 us  [per_device(): far = lax.ppermute(near, 'c', [(0, 1), (1, 0)])]
    all_to_all x2 -> x3, blocking collectives: 56.6 us -> 62.1 us  [from_all(): return lax.all_to_all(copies, axis, split_axis=0, concat_axis=0, tiled=True)]
    all_to_all x2, waiting for transfers between devices: 16.7 us -> 22.1 us  [from_all(): return lax.all_to_all(copies, axis, split_axis=0, concat_axis=0, tiled=True)]
    all_to_all x2, starting transfers between devices: 7.05 us -> 10.7 us  [from_all(): return lax.all_to_all(copies, axis, split_axis=0, concat_axis=0, tiled=True)]
    ppermute x1, starting transfers between devices: 12.8 us -> 9.69 us  [per_device(): got = lax.ppermute(local, ('y', 'mp'), pairs)]
where the time goes in v2:
time: 192 us; the launch traced here: 191 us
  blocking collectives  62.1 us (32%)
  starting transfers between devices  45.7 us (24%)
  waiting for transfers between devices  36.2 us (19%)
  Pallas kernels  16.4 us (9%)
  between operations  13.7 us (7%)
  local copies, waits for them, and re-layouts  7.06 us (4%)
  other arithmetic  6 us (3%)
  matrix products  3.98 us (2%)
    all_to_all x3, blocking collectives, from_all(): return lax.all_to_all(copies, axis, split_axis=0, concat_axis=0, tiled=True)  62.1 us
    all_to_all x2, waiting for transfers between devices, from_all(): return lax.all_to_all(copies, axis, split_axis=0, concat_axis=0, tiled=True)  22.1 us
    ppermute x2, waiting for transfers between devices, swap(): return lax.ppermute(array, 'mp', [(0, 1), (1, 0)])  13.6 us
    ppermute x1, starting transfers between devices, per_device(): far = lax.ppermute(near, 'c', [(0, 1), (1, 0)])  13 us
    ppermute x2, starting transfers between devices, swap(): return lax.ppermute(array, 'mp', [(0, 1), (1, 0)])  12.3 us
    all_to_all x2, starting transfers between devices, from_all(): return lax.all_to_all(copies, axis, split_axis=0, concat_axis=0, tiled=True)  10.7 us
    ppermute x1, starting transfers between devices, per_device(): got = lax.ppermute(local, ('y', 'mp'), pairs)  9.69 us
    pallas_call x1, Pallas kernels, head_kernel(): pl.pallas_call(head_body, out_shape=jax.ShapeDtypeStruct((rows, width), F...  7.67 us
  transfers between devices with their start and end apart: 7, of which 5 were waited for; matrix products, arithmetic and copies ran while one was open for 6% of the time, Pallas kernels for 5%

profile of v2, /device:TPU:1, one launch (start us, length us, event | category | flops | bytes accessed | tf_op | source)
XLA Modules:
  0.0 191.2 jit_solution(14889410738891064918)
XLA Ops:
  6.5 0.0 copy-start.14
  6.5 0.0 all-gather.3.cloned.1.call-start
  6.5 0.8 reshape.65
  7.3 0.8 fusion.24
  8.1 18.5 %all_to_all.25 = bf16[4,32,640]{2,1,0:T(8,128)(2,1)S(1)} all-to-all(bf16[4,32,640]{2,1,0:T(8,128)(2,1)S(1)} %broadcast_in_dim.14), channel_id=1, replica_groups=mesh['y'=8,'zh'=4,'x'=4,'c'=2,'mp'=2] {'zh'}, dimensions={0} | all-to-all | bytes 327680 | tf_op jit(solution)/shard_map/all_to_all | solution.py:74
  26.6 0.0 copy-start.5
  26.6 0.0 copy-start.4
  26.6 0.0 copy-start.10
  26.6 0.0 copy-start.12
  26.6 0.0 copy-start.8
  26.6 0.1 broadcast_in_dim.15
  26.7 11.4 %all_to_all.26 = bf16[4,128,640]{2,1,0:T(8,128)(2,1)S(1)} all-to-all(bf16[4,128,640]{2,1,0:T(8,128)(2,1)S(1)} %broadcast_in_dim.15), channel_id=1, replica_groups=mesh['y'=8,'zh'=4,'x'=4,'c'=2,'mp'=2] {'x'}, dimensions={0} | all-to-all | bytes 1310720 | tf_op jit(solution)/shard_map/all_to_all | solution.py:74
  38.1 0.0 copy-done.14
  38.1 1.4 convolution_convert_fusion
  39.6 0.0 all-gather.3.cloned.1.call-update
  39.6 0.0 copy-done.5
  39.6 0.0 copy-done.4
  39.6 9.7 %collective-permute-start = (bf16[16,640]{1,0:T(8,128)(2,1)S(1)}, bf16[16,640]{1,0:T(8,128)(2,1)S(1)}, u32[]{:S(2)}, u32[]{:S(2)}) collective-permute-start(bf16[16,640]{1,0:T(8,128)(2,1)S(1)} %fusion.29), channel_id=1, source_target_pairs={{0,257},{1,256},{64,321},{65,320},{128,385},{129,384},{192,449},{1... | collective-permute-start | bytes 61448 | tf_op jit(solution)/shard_map/ppermute | solution.py:329
  49.4 0.0 copy-done.10
  49.4 0.1 iota_add_fusion
  49.4 0.0 copy-done.9
  49.5 0.0 copy-done.12
  49.5 0.1 reshape_tile.3.scale_ref
  49.6 0.0 copy-done.8
  49.6 0.3 reshape.70
  49.9 0.2 reshape.71.gain_ref
  50.1 0.4 collective-permute-done
  50.5 0.7 broadcast_in_dim.16
  51.3 5.4 %all-to-all-start.2 = ((bf16[8,24,640]{2,1,0:T(8,128)(2,1)}), bf16[8,24,640]{2,1,0:T(8,128)(2,1)S(1)}, u32[]{:S(2)}, u32[]{:S(2)}) async-start(bf16[8,24,640]{2,1,0:T(8,128)(2,1)} %broadcast_in_dim.16), calls=%async_computation.2 | async-start | bytes 491520 | tf_op jit(solution)/shard_map/all_to_all | solution.py:74
  56.7 0.1 fusion.14.pool_ref
  56.9 0.0 copy-start.7
  56.9 1.1 compare_convert_fusion.1.last_hbm
  58.0 10.6 %all-to-all-done.2 = bf16[8,24,640]{2,1,0:T(8,128)(2,1)S(1)} async-done(((bf16[8,24,640]{2,1,0:T(8,128)(2,1)}), bf16[8,24,640]{2,1,0:T(8,128)(2,1)S(1)}, u32[]{:S(2)}, u32[]{:S(2)}) %all-to-all-start.2) | async-done | bytes 245792 | tf_op jit(solution)/shard_map/all_to_all | solution.py:74
  68.6 1.0 broadcast_in_dim.19
  69.7 5.3 %all-to-all-start.3 = ((bf16[4,192,640]{2,1,0:T(8,128)(2,1)}), bf16[4,192,640]{2,1,0:T(8,128)(2,1)S(1)}, u32[]{:S(2)}, u32[]{:S(2)}) async-start(bf16[4,192,640]{2,1,0:T(8,128)(2,1)} %broadcast_in_dim.19), calls=%async_computation.3 | async-start | bytes 1966080 | tf_op jit(solution)/shard_map/all_to_all | solution.py:74
  75.0 0.0 copy-done.3
  75.0 0.1 fusion.7
  75.1 0.0 copy-done.6
  75.1 0.1 fusion.9
  75.3 0.0 copy-done.7
  75.3 1.5 fusion.3
  76.8 0.9 fusion.34
  77.7 3.5 %fusion.1 = (bf16[1280,1280]{1,0:T(8,128)(2,1)}, bf16[1280,1280]{1,0:T(8,128)(2,1)}) fusion(s32[1280]{0:T(1024)S(1)} %copy-done.7, s32[1280]{0:T(1024)S(1)} %pad_add_fusion), kind=kLoop, calls=%fused_computation.3 | loop fusion | flops 6553600 | bytes 6563840 | tf_op jit(solution)/shard_map/convert_element_type | solution.py:358
  81.2 11.5 %all-to-all-done.3 = bf16[4,192,640]{2,1,0:T(8,128)(2,1)S(1)} async-done(((bf16[4,192,640]{2,1,0:T(8,128)(2,1)}), bf16[4,192,640]{2,1,0:T(8,128)(2,1)S(1)}, u32[]{:S(2)}, u32[]{:S(2)}) %all-to-all-start.3) | async-done | bytes 983072 | tf_op jit(solution)/shard_map/all_to_all | solution.py:74
  92.7 0.0 copy-done.13
  92.7 1.0 fusion.5
  93.7 0.0 copy-done.11
  93.8 0.1 broadcast_in_dim.17.valid_ref
  93.8 0.3 broadcast_in_dim.20
  94.1 32.2 %all_to_all.27.near_hbm = bf16[4,640,640]{2,1,0:T(8,128)(2,1)} all-to-all(bf16[4,640,640]{2,1,0:T(8,128)(2,1)S(1)} %broadcast_in_dim.20), channel_id=1, replica_groups=mesh['y'=8,'zh'=4,'x'=4,'c'=2,'mp'=2] {'x'}, dimensions={0} | all-to-all | bytes 6553600 | tf_op jit(solution)/shard_map/all_to_all | solution.py:74
  126.3 13.0 %collective-permute-start.3 = (bf16[4,640,640]{2,1,0:T(8,128)(2,1)}, bf16[4,640,640]{2,1,0:T(8,128)(2,1)S(1)}, u32[]{:S(2)}, u32[]{:S(2)}) collective-permute-start(bf16[4,640,640]{2,1,0:T(8,128)(2,1)} %all_to_all.27.near_hbm), channel_id=1, source_target_pairs={{0,2},{2,0},{1,3},{3,1},{4,6},{6,4},{5,7},{7,5},{8,10},{10,8},{9,1... | collective-permute-start | bytes 9830408 | tf_op jit(solution)/shard_map/ppermute | solution.py:375
  139.3 0.0 all-gather.3.cloned.1.call-done
  139.3 0.0 copy-start.1
  139.3 1.6 copy-done.1
  140.9 1.0 copy-done.2
  141.9 7.7 %attend.1 = (bf16[112,1280]{1,0:T(8,128)(2,1)S(1)}, bf16[2,16,80,640]{3,2,1,0:T(8,128)(2,1)S(1)}) custom-call(bf16[112,1280]{1,0:T(8,128)(2,1)S(1)} %copy-done.2, f32[1,640]{1,0:T(1,128)S(1)} %reshape_tile.3.scale_ref, s32[112,128]{1,0:T(8,128)S(1)} %broadcast_in_dim.17.valid_ref, bf16[640,128]{1,0:T(8,128)(2,1)S(1)} %fusion.14.pool_ref, ...), custom_call_target="tpu_custom_call" | custom-call | tf_op jit(solution)/shard_map/attend/pallas_call | solution.py:167
  149.6 9.0 %collective-permute-start.1 = (bf16[112,1280]{1,0:T(8,128)(2,1)S(1)}, bf16[112,1280]{1,0:T(8,128)(2,1)S(1)}, u32[]{:S(2)}, u32[]{:S(2)}) collective-permute-start(bf16[112,1280]{1,0:T(8,128)(2,1)S(1)} %get-tuple-element.29.own_ref.own1_ref), channel_id=1, source_target_pairs={{0,1},{1,0},{2,3},{3,2},{4,5},{5,4},{6,7},{7,6},{8,9},{9,8},{10,11... | collective-permute-start | bytes 860168 | tf_op jit(solution)/shard_map/ppermute | solution.py:303
  158.6 7.2 %collective-permute-done.1.other_ref.other1_ref = bf16[112,1280]{1,0:T(8,128)(2,1)S(1)} collective-permute-done((bf16[112,1280]{1,0:T(8,128)(2,1)S(1)}, bf16[112,1280]{1,0:T(8,128)(2,1)S(1)}, u32[]{:S(2)}, u32[]{:S(2)}) %collective-permute-start.1) | collective-permute-done | bytes 286752 | tf_op jit(solution)/shard_map/ppermute | solution.py:303
  165.8 0.0 copy-done
  165.8 1.1 mlp.1.own2_ref
  166.9 3.3 %collective-permute-start.2 = (bf16[112,1280]{1,0:T(8,128)(2,1)S(1)}, bf16[112,1280]{1,0:T(8,128)(2,1)S(1)}, u32[]{:S(2)}, u32[]{:S(2)}) collective-permute-start(bf16[112,1280]{1,0:T(8,128)(2,1)S(1)} %mlp.1.own2_ref), channel_id=1, source_target_pairs={{0,1},{1,0},{2,3},{3,2},{4,5},{5,4},{6,7},{7,6},{8,9},{9,8},{10,11... | collective-permute-start | bytes 860168 | tf_op jit(solution)/shard_map/ppermute | solution.py:303
  170.2 0.0 collective-permute-done.3.far_ref
  170.2 6.4 %collective-permute-done.2.other2_ref = bf16[112,1280]{1,0:T(8,128)(2,1)S(1)} collective-permute-done((bf16[112,1280]{1,0:T(8,128)(2,1)S(1)}, bf16[112,1280]{1,0:T(8,128)(2,1)S(1)}, u32[]{:S(2)}, u32[]{:S(2)}) %collective-permute-start.2) | collective-permute-done | bytes 286752 | tf_op jit(solution)/shard_map/ppermute | solution.py:303
  176.6 7.7 %head.1 = f32[112,640]{1,0:T(8,128)} custom-call(bf16[112,1280]{1,0:T(8,128)(2,1)S(1)} %copy-done, bf16[112,1280]{1,0:T(8,128)(2,1)S(1)} %get-tuple-element.29.own_ref.own1_ref, bf16[112,1280]{1,0:T(8,128)(2,1)S(1)} %collective-permute-done.1.other_ref.other1_ref, bf16[112,1280]{1,0:T(8,128)(2,1)S(1)} %mlp.1.own2_ref, ...), custom_call_target="tpu_custom_call" | custom-call | tf_op jit(solution)/shard_map/head/pallas_call | solution.py:277
  (22 shorter events, 0.2 us)
Async XLA Ops:
  6.5 31.6 %copy-start.14 = (s32[480]{0:T(512)S(1)}, s32[480]{0:T(512)}, u32[]{:S(2)}) copy-start(s32[480]{0:T(512)} %constant.48.clone) | copy-start | bytes 5764
  6.5 132.8 %all-gather.3.cloned.1.call-start = ((), (), s32[]{:S(2)}) async-start(), calls=%async_computation.5 | async-start | bytes 10444800 | tf_op jit(solution)/shard_map/all_gather | solution.py:343
  26.6 13.0 %copy-start.5 = (bf16[2,640,5]{1,0,2:T(2,128)(2,1)S(1)}, bf16[2,640,5]{1,0,2:T(2,128)(2,1)}, u32[]{:S(2)}) copy-start(bf16[2,640,5]{1,0,2:T(2,128)(2,1)} %param.30) | copy-start | bytes 38404
  26.6 13.1 %copy-start.4 = (bf16[5,640]{1,0:T(8,128)(2,1)S(1)}, bf16[5,640]{1,0:T(8,128)(2,1)}, u32[]{:S(2)}) copy-start(bf16[5,640]{1,0:T(8,128)(2,1)} %param.29) | copy-start | bytes 19204
  26.6 22.8 %copy-start.10 = (s32[320]{0:T(512)S(1)}, s32[320]{0:T(512)}, u32[]{:S(2)}) copy-start(s32[320]{0:T(512)} %constant.52.clone) | copy-start | bytes 3844
  26.6 22.9 %copy-start.9 = (s32[640]{0:T(1024)S(1)}, s32[640]{0:T(1024)}, u32[]{:S(2)}) copy-start(s32[640]{0:T(1024)} %constant.51.clone) | copy-start | bytes 7684
  26.6 22.9 %copy-start.12 = (f32[80]{0:T(128)S(1)}, f32[80]{0:T(128)}, u32[]{:S(2)}) copy-start(f32[80]{0:T(128)} %param.24) | copy-start | bytes 964
  26.6 23.0 %copy-start.8 = (f32[1280]{0:T(1024)S(1)}, f32[1280]{0:T(1024)}, u32[]{:S(2)}) copy-start(f32[1280]{0:T(1024)} %param.23) | copy-start | bytes 15364
  39.6 10.8 %collective-permute-start = (bf16[16,640]{1,0:T(8,128)(2,1)S(1)}, bf16[16,640]{1,0:T(8,128)(2,1)S(1)}, u32[]{:S(2)}, u32[]{:S(2)}) collective-permute-start(bf16[16,640]{1,0:T(8,128)(2,1)S(1)} %fusion.29), channel_id=1, source_target_pairs={{0,257},{1,256},{64,321},{65,320},{128,385},{129,384},{192,449},{1... | collective-permute-start | bytes 61448 | tf_op jit(solution)/shard_map/ppermute | solution.py:329
  51.3 23.7 %copy-start.3 = (bf16[112,1280]{1,0:T(8,128)(2,1)S(1)}, bf16[112,1280]{1,0:T(8,128)(2,1)}, u32[]{:S(2)}) copy-start(bf16[112,1280]{1,0:T(8,128)(2,1)} %param.18) | copy-start | bytes 860164
  51.3 17.4 %all-to-all-start.2 = ((bf16[8,24,640]{2,1,0:T(8,128)(2,1)}), bf16[8,24,640]{2,1,0:T(8,128)(2,1)S(1)}, u32[]{:S(2)}, u32[]{:S(2)}) async-start(bf16[8,24,640]{2,1,0:T(8,128)(2,1)} %broadcast_in_dim.16), calls=%async_computation.2 | async-start | bytes 491520 | tf_op jit(solution)/shard_map/all_to_all | solution.py:74
  56.7 18.4 %copy-start.6 = (f32[1280]{0:T(1024)S(1)}, f32[1280]{0:T(1024)}, u32[]{:S(2)}) copy-start(f32[1280]{0:T(1024)} %param.22) | copy-start | bytes 15364
  56.9 18.4 %copy-start.7 = (s32[1280]{0:T(1024)S(1)}, s32[1280]{0:T(1024)}, u32[]{:S(2)}) copy-start(s32[1280]{0:T(1024)} %constant.49.clone) | copy-start | bytes 15364
  69.7 23.0 %all-to-all-start.3 = ((bf16[4,192,640]{2,1,0:T(8,128)(2,1)}), bf16[4,192,640]{2,1,0:T(8,128)(2,1)S(1)}, u32[]{:S(2)}, u32[]{:S(2)}) async-start(bf16[4,192,640]{2,1,0:T(8,128)(2,1)} %broadcast_in_dim.19), calls=%async_computation.3 | async-start | bytes 1966080 | tf_op jit(solution)/shard_map/all_to_all | solution.py:74
  77.7 15.0 %copy-start.13 = (s32[640]{0:T(1024)S(1)}, s32[640]{0:T(1024)}, u32[]{:S(2)}) copy-start(s32[640]{0:T(1024)} %constant.50.clone) | copy-start | bytes 7684
  81.2 12.6 %copy-start.11 = (s32[112]{0:T(128)S(1)}, s32[112]{0:T(128)}, u32[]{:S(2)}) copy-start(s32[112]{0:T(128)} %param.21) | copy-start | bytes 1348
  126.3 43.9 %collective-permute-start.3 = (bf16[4,640,640]{2,1,0:T(8,128)(2,1)}, bf16[4,640,640]{2,1,0:T(8,128)(2,1)S(1)}, u32[]{:S(2)}, u32[]{:S(2)}) collective-permute-start(bf16[4,640,640]{2,1,0:T(8,128)(2,1)} %all_to_all.27.near_hbm), channel_id=1, source_target_pairs={{0,2},{2,0},{1,3},{3,1},{4,6},{6,4},{5,7},{7,5},{8,10},{10,8},{9,1... | collective-permute-start | bytes 9830408 | tf_op jit(solution)/shard_map/ppermute | solution.py:375
  139.3 1.6 copy-start.1
  140.9 1.0 copy-start.2
  141.9 23.9 %copy-start = (bf16[112,1280]{1,0:T(8,128)(2,1)S(1)}, bf16[112,1280]{1,0:T(8,128)(2,1)}, u32[]{:S(2)}) copy-start(bf16[112,1280]{1,0:T(8,128)(2,1)} %get-tuple-element.24.stream_ref) | copy-start | bytes 860164
  149.6 16.2 %collective-permute-start.1 = (bf16[112,1280]{1,0:T(8,128)(2,1)S(1)}, bf16[112,1280]{1,0:T(8,128)(2,1)S(1)}, u32[]{:S(2)}, u32[]{:S(2)}) collective-permute-start(bf16[112,1280]{1,0:T(8,128)(2,1)S(1)} %get-tuple-element.29.own_ref.own1_ref), channel_id=1, source_target_pairs={{0,1},{1,0},{2,3},{3,2},{4,5},{5,4},{6,7},{7,6},{8,9},{9,8},{10,11... | collective-permute-start | bytes 860168 | tf_op jit(solution)/shard_map/ppermute | solution.py:303
  166.9 9.7 %collective-permute-start.2 = (bf16[112,1280]{1,0:T(8,128)(2,1)S(1)}, bf16[112,1280]{1,0:T(8,128)(2,1)S(1)}, u32[]{:S(2)}, u32[]{:S(2)}) collective-permute-start(bf16[112,1280]{1,0:T(8,128)(2,1)S(1)} %mlp.1.own2_ref), channel_id=1, source_target_pairs={{0,1},{1,0},{2,3},{3,2},{4,5},{5,4},{6,7},{7,6},{8,9},{9,8},{10,11... | collective-permute-start | bytes 860168 | tf_op jit(solution)/shard_map/ppermute | solution.py:303
Sparse Core Ops, SparseCore 0:
  39.7 70.6 all-gather.2

commit v3 on v2

--- a/solution.py
+++ b/solution.py
@@ -38,19 +38,33 @@
     return f.transpose(2, 1, 0, 3).reshape(D // 2 // NC).astype(np.int32)
 
 
-def output_rows(padded):
-    zh, y, piece = np.meshgrid(np.arange(NZ), np.arange(NY), np.arange(PIECE), indexing="ij")
-
-    def at(slot, row):
-        return (zh * NY + slot) * padded + row + piece
-
-    def halves(row):
-        src = at(y, row)
-        return np.concatenate([src[:, : NY // 2].reshape(-1), src[:, NY // 2 :].reshape(-1)])
-
-    own = at(y, 0).reshape(-1)
-    other = at((y + NY // 2) % NY, PIECE).reshape(-1)
-    return np.concatenate([own, other, halves(2 * PIECE), halves(3 * PIECE)])
+def first_rows(padded):
+    y, piece = np.meshgrid(np.arange(NY), np.arange(PIECE), indexing="ij")
+
+    def hidden(half):
+        return ((y * 2 + half) * padded + piece).reshape(-1)
+
+    def final(k):
+        lower = y[: NY // 2], piece[: NY // 2]
+        return np.concatenate(
+            [((lower[0] * 2 + half) * padded + k * PIECE + lower[1]).reshape(-1) for half in range(2)]
+        )
+
+    rows = np.concatenate([hidden(0), hidden(1), final(1), final(2)])
+    step = np.repeat([0, NY * padded], NY * 2 * PIECE)
+    return rows.astype(np.int32), step.astype(np.int32)
+
+
+def second_rows():
+    each = NY * PIECE
+    zh = np.arange(NZ)[:, None]
+
+    def block(start, count):
+        return (zh * 4 * each + start + np.arange(count)[None, :]).reshape(-1)
+
+    whole = [block(n * each, each) for n in range(2)]
+    halves = [block(n * (each // 2), each // 2) for n in range(4, 8)]
+    return np.concatenate(whole + halves)
 
 
 def matrix_rows(places, padded):
@@ -60,7 +74,7 @@
 
 
 def one_hot(src, count):
-    src = jnp.asarray(src.astype(np.int32))
+    src = jnp.asarray(src, jnp.int32)
     return (src[:, None] == jnp.arange(count, dtype=jnp.int32)[None, :]).astype(BF16)
 
 
@@ -206,7 +220,7 @@
 
 
 def head_body(
-    stream_ref, own1_ref, other1_ref, own2_ref, other2_ref, first_ref, far_ref,
+    stream_ref, own1_ref, other1_ref, own2_ref, other2_ref, far_ref,
     turn_hbm, plain_hbm, last_hbm, near_hbm,
     out_ref, turn_buf, plain_buf, last_buf, near_ref, sems,
 ):
@@ -245,10 +259,7 @@
         pre = pre + dot(turned[:, half:], part(far_ref, start, each))
         return (pre / (1.0 + jnp.exp(-pre))).astype(BF16)
 
-    act_own = hidden(0)
-    act_other = hidden(each)
-    first = first_ref[...] > 0
-    act = (jnp.where(first, act_own, act_other), jnp.where(first, act_other, act_own))
+    act = (hidden(0), hidden(each))
     load_plain.wait()
     plain = dot(s2, plain_buf[...]).astype(BF16)
     skip = (plain[:, :width], plain[:, width:])
@@ -269,7 +280,7 @@
     out_ref[...] = dot(high, last_buf[...]) + dot(low, last_buf[...])
 
 
-def head_kernel(stream, own1, other1, own2, other2, first, turn, plain, last, near, far):
+def head_kernel(stream, own1, other1, own2, other2, turn, plain, last, near, far):
     rows = stream.shape[0]
     width = near.shape[-1]
     vmem = pl.BlockSpec(memory_space=pltpu.VMEM)
@@ -277,7 +288,7 @@
     return pl.pallas_call(
         head_body,
         out_shape=jax.ShapeDtypeStruct((rows, width), F32),
-        in_specs=[vmem] * 7 + [hbm] * 4,
+        in_specs=[vmem] * 6 + [hbm] * 4,
         out_specs=vmem,
         scratch_shapes=[
             pltpu.VMEM(turn.shape, BF16),
@@ -289,7 +300,7 @@
         compiler_params=pltpu.CompilerParams(vmem_limit_bytes=32 * 2**20),
         name="head",
     )(
-        stream, own1, other1, own2, other2, first, in_vmem(far),
+        stream, own1, other1, own2, other2, in_vmem(far),
         in_hbm(turn), in_hbm(plain), in_hbm(last), in_hbm(near),
     )
 
@@ -321,22 +332,17 @@
     rows, _, width = context_key_cache.shape
     heads = width // HD
     piece = np.arange(PIECE)
-    y, core, mp = (lax.axis_index(axis) for axis in ("y", "c", "mp"))
-    local = padded_rows(
+    core, mp = lax.axis_index("c"), lax.axis_index("mp")
+    second = padded_rows(
         [head_hidden, jnp.transpose(final_layer_matrices, (0, 2, 1)).reshape(2 * PIECE, width)]
     )
-    pairs = [(2 * a + m, 2 * ((a + NY // 2) % NY) + 1 - m) for a in range(NY) for m in range(2)]
-    got = lax.ppermute(local, ("y", "mp"), pairs)
-    keep = (y < NY // 2) == (mp == 0)
-    finals = jnp.where(keep, local[PIECE : 3 * PIECE], got[PIECE : 3 * PIECE])
-    second = padded_rows([local[:PIECE], got[:PIECE], finals])
     first = padded_rows(
         [jnp.transpose(w_qkv, (1, 0, 2)).reshape(3 * PIECE, width), w_out.T, w_up, w_down.T]
     )
     places = np.stack([piece * 3 + b for b in range(3)] + [piece + PIECE * b for b in range(3, 6)])
     shared = from_all(first, "zh").reshape(-1, width)
     shared = from_all(shared, "x").reshape(-1, width)
-    shared2 = from_all(second, "y").reshape(-1, width)
+    shared2 = from_all(second, ("y", "mp")).reshape(-1, width)
     pick = one_hot(matrix_rows(places, first.shape[0]), shared.shape[0])
     block1 = dot(pick, shared).astype(BF16)
     order = jnp.asarray(feature_order())
@@ -344,9 +350,11 @@
     _, shared2, new_embed, order = lax.optimization_barrier(
         (block1, shared2, new_embed, order)
     )
+    src, step = first_rows(second.shape[0])
+    pick = one_hot(jnp.asarray(src) + jnp.asarray(step) * mp, shared2.shape[0])
+    shared2 = dot(pick, shared2).astype(BF16)
     shared2 = from_all(shared2, "zh").reshape(-1, width)
-    pick = one_hot(output_rows(second.shape[0]), shared2.shape[0])
-    block2 = dot(pick, shared2).astype(BF16)
+    block2 = dot(one_hot(second_rows(), shared2.shape[0]), shared2).astype(BF16)
 
     half = jnp.asarray(half_order())
     order2 = jnp.concatenate([half + PIECE * core, half + PIECE * (1 - core)])
@@ -365,10 +373,9 @@
     pool = (jnp.arange(width)[:, None] // HD == jnp.arange(128)[None, :]).astype(BF16)
     scale = jnp.tile(query_scale, heads).reshape(1, width)
     used = jnp.broadcast_to(valid[:, None], (rows, 128))
-    is_first = jnp.broadcast_to((mp == 0).astype(F32), (1, width))
-    normed_o, stream_o, gain_o, pool, scale, used, is_first, turn, plain, last, block2 = (
+    normed_o, stream_o, gain_o, pool, scale, used, turn, plain, last, block2 = (
         lax.optimization_barrier(
-            (normed_o, stream_o, gain_o, pool, scale, used, is_first, turn, plain, last, block2)
+            (normed_o, stream_o, gain_o, pool, scale, used, turn, plain, last, block2)
         )
     )
     near = from_all(block2, "x")
@@ -381,7 +388,7 @@
     part2 = mlp_kernel(stream_o, part1, other1, gain_o, feed_w)
     other2 = swap(part2)
     return head_kernel(
-        stream_o, part1, other1, part2, other2, is_first, turn, plain, last, near, far
+        stream_o, part1, other1, part2, other2, turn, plain, last, near, far
     )
 
 

time: 192 us -> 177 us (0.922)
  starting transfers between devices: 45.7 us -> 22.1 us
  blocking collectives: 62.1 us -> 75.3 us
  waiting for transfers between devices: 36.2 us -> 31 us
    all_to_all x3, blocking collectives: 62.1 us -> 75.3 us  [from_all(): return lax.all_to_all(copies, axis, split_axis=0, concat_axis=0, tiled=True)]
    ppermute x1 -> x0, starting transfers between devices: 9.69 us -> none  [per_device(): got = lax.ppermute(local, ('y', 'mp'), pairs)]
    ppermute x2, starting transfers between devices: 12.3 us -> 4.3 us  [swap(): return lax.ppermute(array, 'mp', [(0, 1), (1, 0)])]
    ppermute x1, starting transfers between devices: 13 us -> 5.11 us  [per_device(): far = lax.ppermute(near, 'c', [(0, 1), (1, 0)])]
    all_to_all x2, waiting for transfers between devices: 22.1 us -> 15.6 us  [from_all(): return lax.all_to_all(copies, axis, split_axis=0, concat_axis=0, tiled=True)]
    all_to_all x2, starting transfers between devices: 10.7 us -> 12.7 us  [from_all(): return lax.all_to_all(copies, axis, split_axis=0, concat_axis=0, tiled=True)]
    dot_general x3 -> x4, matrix products: 3.98 us -> 4.15 us  [dot(): return jnp.dot(a, b, preferred_element_type=F32)]
  transfers between devices with their start and end apart: 7 -> 6, of which waited for: 5 -> 4; matrix products, arithmetic and copies ran while one was open for 6% -> 7% of each run, Pallas kernels for 5% -> 5%
where the time goes in v3:
time: 177 us; the launch traced here: 176 us
  blocking collectives  75.3 us (43%)
  waiting for transfers between devices  31 us (18%)
  starting transfers between devices  22.1 us (12%)
  Pallas kernels  16.4 us (9%)
  between operations  13.8 us (8%)
  local copies, waits for them, and re-layouts  7.07 us (4%)
  other arithmetic  6.03 us (3%)
  matrix products  4.15 us (2%)
    all_to_all x3, blocking collectives, from_all(): return lax.all_to_all(copies, axis, split_axis=0, concat_axis=0, tiled=True)  75.3 us
    all_to_all x2, waiting for transfers between devices, from_all(): return lax.all_to_all(copies, axis, split_axis=0, concat_axis=0, tiled=True)  15.6 us
    ppermute x2, waiting for transfers between devices, swap(): return lax.ppermute(array, 'mp', [(0, 1), (1, 0)])  15.3 us
    all_to_all x2, starting transfers between devices, from_all(): return lax.all_to_all(copies, axis, split_axis=0, concat_axis=0, tiled=True)  12.7 us
    pallas_call x1, Pallas kernels, head_kernel(): pl.pallas_call(head_body, out_shape=jax.ShapeDtypeStruct((rows, width), F...  7.67 us
    pallas_call x1, Pallas kernels, attention_kernel(): pl.pallas_call(attention_body, out_shape=(pltpu.VMEM((rows, D), BF16), pl...  7.66 us
    ppermute x1, starting transfers between devices, per_device(): far = lax.ppermute(near, 'c', [(0, 1), (1, 0)])  5.11 us
    ppermute x2, starting transfers between devices, swap(): return lax.ppermute(array, 'mp', [(0, 1), (1, 0)])  4.3 us
  transfers between devices with their start and end apart: 6, of which 4 were waited for; matrix products, arithmetic and copies ran while one was open for 7% of the time, Pallas kernels for 5%

profile of v3, /device:TPU:1, one launch (start us, length us, event | category | flops | bytes accessed | tf_op | source)
XLA Modules:
  0.0 175.9 jit_solution(7481402683778313281)
XLA Ops:
  6.5 0.0 all-gather.3.cloned.1.call-start
  6.5 0.8 reshape.66
  7.3 0.8 fusion.22
  8.1 18.5 %all_to_all.25 = bf16[4,32,640]{2,1,0:T(8,128)(2,1)S(1)} all-to-all(bf16[4,32,640]{2,1,0:T(8,128)(2,1)S(1)} %broadcast_in_dim.12), channel_id=1, replica_groups=mesh['y'=8,'zh'=4,'x'=4,'c'=2,'mp'=2] {'zh'}, dimensions={0} | all-to-all | bytes 327680 | tf_op jit(solution)/shard_map/all_to_all | solution.py:88
  26.6 0.1 broadcast_in_dim.13
  26.6 0.0 copy-start.10
  26.6 0.0 copy-start.11
  26.6 0.0 copy-start.12
  26.7 0.0 copy-start.9
  26.7 0.0 copy-start.14
  26.7 0.0 copy-start.8
  26.7 11.6 %all_to_all.26 = bf16[4,128,640]{2,1,0:T(8,128)(2,1)S(1)} all-to-all(bf16[4,128,640]{2,1,0:T(8,128)(2,1)S(1)} %broadcast_in_dim.13), channel_id=1, replica_groups=mesh['y'=8,'zh'=4,'x'=4,'c'=2,'mp'=2] {'x'}, dimensions={0} | all-to-all | bytes 1310720 | tf_op jit(solution)/shard_map/all_to_all | solution.py:88
  38.3 0.0 copy-done.16
  38.3 1.4 convolution_convert_fusion
  39.7 0.0 all-gather.3.cloned.1.call-update
  39.8 0.0 copy-done.4
  39.8 0.0 copy-done.5
  39.8 0.8 broadcast_in_dim.14
  40.6 9.2 %all-to-all-start.2 = ((bf16[16,16,640]{2,1,0:T(8,128)(2,1)}), bf16[16,16,640]{2,1,0:T(8,128)(2,1)S(1)}, u32[]{:S(2)}, u32[]{:S(2)}) async-start(bf16[16,16,640]{2,1,0:T(8,128)(2,1)} %broadcast_in_dim.14), calls=%async_computation.2 | async-start | bytes 655360 | tf_op jit(solution)/shard_map/all_to_all | solution.py:88
  49.8 0.0 copy-done.10
  49.8 0.1 iota_add_fusion
  49.9 0.0 copy-done.11
  49.9 0.0 copy-done.12
  49.9 0.0 copy-done.9
  49.9 0.0 copy-done.14
  49.9 0.1 reshape_tile.3.scale_ref
  50.0 0.0 copy-done.8
  50.0 0.3 reshape.71
  50.3 0.0 copy-start.3
  50.3 0.0 copy-start.6
  50.4 0.2 reshape.72.gain_ref
  50.6 0.1 fusion.14.pool_ref
  50.8 0.0 copy-start.7
  50.8 1.1 compare_convert_fusion.1.last_hbm
  51.9 8.1 %all-to-all-done.2 = bf16[16,16,640]{2,1,0:T(8,128)(2,1)S(1)} async-done(((bf16[16,16,640]{2,1,0:T(8,128)(2,1)}), bf16[16,16,640]{2,1,0:T(8,128)(2,1)S(1)}, u32[]{:S(2)}, u32[]{:S(2)}) %all-to-all-start.2) | async-done | bytes 327712 | tf_op jit(solution)/shard_map/all_to_all | solution.py:88
  59.9 0.3 convolution_convert_fusion.1
  60.2 1.0 broadcast_in_dim.16
  61.2 3.5 %all-to-all-start.3 = ((bf16[4,160,640]{2,1,0:T(8,128)(2,1)}), bf16[4,160,640]{2,1,0:T(8,128)(2,1)S(1)}, u32[]{:S(2)}, u32[]{:S(2)}) async-start(bf16[4,160,640]{2,1,0:T(8,128)(2,1)} %broadcast_in_dim.16), calls=%async_computation.3 | async-start | bytes 1638400 | tf_op jit(solution)/shard_map/all_to_all | solution.py:88
  64.7 0.0 copy-done.3
  64.7 0.1 fusion.7
  64.8 0.0 copy-done.6
  64.9 0.1 fusion.9
  65.0 1.5 fusion.3
  66.5 0.9 fusion.30
  67.4 3.6 %fusion.1 = (bf16[1280,1280]{1,0:T(8,128)(2,1)}, bf16[1280,1280]{1,0:T(8,128)(2,1)}) fusion(s32[1280]{0:T(1024)S(1)} %copy-done.7, s32[1280]{0:T(1024)S(1)} %pad_add_fusion), kind=kLoop, calls=%fused_computation.3 | loop fusion | flops 6553600 | bytes 6563840 | tf_op jit(solution)/shard_map/convert_element_type | solution.py:366
  71.0 7.6 %all-to-all-done.3 = bf16[4,160,640]{2,1,0:T(8,128)(2,1)S(1)} async-done(((bf16[4,160,640]{2,1,0:T(8,128)(2,1)}), bf16[4,160,640]{2,1,0:T(8,128)(2,1)S(1)}, u32[]{:S(2)}, u32[]{:S(2)}) %all-to-all-start.3) | async-done | bytes 819232 | tf_op jit(solution)/shard_map/all_to_all | solution.py:88
  78.6 0.9 fusion.5
  79.5 0.1 broadcast_in_dim.15.valid_ref
  79.6 0.3 broadcast_in_dim.17
  79.9 45.3 %all_to_all.27.near_hbm = bf16[4,640,640]{2,1,0:T(8,128)(2,1)} all-to-all(bf16[4,640,640]{2,1,0:T(8,128)(2,1)S(1)} %broadcast_in_dim.17), channel_id=1, replica_groups=mesh['y'=8,'zh'=4,'x'=4,'c'=2,'mp'=2] {'x'}, dimensions={0} | all-to-all | bytes 6553600 | tf_op jit(solution)/shard_map/all_to_all | solution.py:88
  125.2 5.1 %collective-permute-start.2 = (bf16[4,640,640]{2,1,0:T(8,128)(2,1)}, bf16[4,640,640]{2,1,0:T(8,128)(2,1)S(1)}, u32[]{:S(2)}, u32[]{:S(2)}) collective-permute-start(bf16[4,640,640]{2,1,0:T(8,128)(2,1)} %all_to_all.27.near_hbm), channel_id=1, source_target_pairs={{0,2},{2,0},{1,3},{3,1},{4,6},{6,4},{5,7},{7,5},{8,10},{10,8},{9,1... | collective-permute-start | bytes 9830408 | tf_op jit(solution)/shard_map/ppermute | solution.py:382
  130.3 0.0 all-gather.3.cloned.1.call-done
  130.3 0.0 copy-start.1
  130.3 1.6 copy-done.1
  132.0 1.0 copy-done.2
  132.9 7.7 %attend.1 = (bf16[112,1280]{1,0:T(8,128)(2,1)S(1)}, bf16[2,16,80,640]{3,2,1,0:T(8,128)(2,1)S(1)}) custom-call(bf16[112,1280]{1,0:T(8,128)(2,1)S(1)} %copy-done.2, f32[1,640]{1,0:T(1,128)S(1)} %reshape_tile.3.scale_ref, s32[112,128]{1,0:T(8,128)S(1)} %broadcast_in_dim.15.valid_ref, bf16[640,128]{1,0:T(8,128)(2,1)S(1)} %fusion.14.pool_ref, ...), custom_call_target="tpu_custom_call" | custom-call | tf_op jit(solution)/shard_map/attend/pallas_call | solution.py:181
  140.6 1.9 %collective-permute-start = (bf16[112,1280]{1,0:T(8,128)(2,1)S(1)}, bf16[112,1280]{1,0:T(8,128)(2,1)S(1)}, u32[]{:S(2)}, u32[]{:S(2)}) collective-permute-start(bf16[112,1280]{1,0:T(8,128)(2,1)S(1)} %get-tuple-element.28.own_ref.own1_ref), channel_id=1, source_target_pairs={{0,1},{1,0},{2,3},{3,2},{4,5},{5,4},{6,7},{7,6},{8,9},{9,8},{10,11... | collective-permute-start | bytes 860168 | tf_op jit(solution)/shard_map/ppermute | solution.py:314
  142.5 8.3 %collective-permute-done.other_ref.other1_ref = bf16[112,1280]{1,0:T(8,128)(2,1)S(1)} collective-permute-done((bf16[112,1280]{1,0:T(8,128)(2,1)S(1)}, bf16[112,1280]{1,0:T(8,128)(2,1)S(1)}, u32[]{:S(2)}, u32[]{:S(2)}) %collective-permute-start) | collective-permute-done | bytes 286752 | tf_op jit(solution)/shard_map/ppermute | solution.py:314
  150.9 0.0 copy-done
  150.9 1.1 mlp.1.own2_ref
  152.0 2.4 %collective-permute-start.1 = (bf16[112,1280]{1,0:T(8,128)(2,1)S(1)}, bf16[112,1280]{1,0:T(8,128)(2,1)S(1)}, u32[]{:S(2)}, u32[]{:S(2)}) collective-permute-start(bf16[112,1280]{1,0:T(8,128)(2,1)S(1)} %mlp.1.own2_ref), channel_id=1, source_target_pairs={{0,1},{1,0},{2,3},{3,2},{4,5},{5,4},{6,7},{7,6},{8,9},{9,8},{10,11... | collective-permute-start | bytes 860168 | tf_op jit(solution)/shard_map/ppermute | solution.py:314
  154.4 0.0 collective-permute-done.2.far_ref
  154.4 7.0 %collective-permute-done.1.other2_ref = bf16[112,1280]{1,0:T(8,128)(2,1)S(1)} collective-permute-done((bf16[112,1280]{1,0:T(8,128)(2,1)S(1)}, bf16[112,1280]{1,0:T(8,128)(2,1)S(1)}, u32[]{:S(2)}, u32[]{:S(2)}) %collective-permute-start.1) | collective-permute-done | bytes 286752 | tf_op jit(solution)/shard_map/ppermute | solution.py:314
  161.4 7.7 %head.1 = f32[112,640]{1,0:T(8,128)} custom-call(bf16[112,1280]{1,0:T(8,128)(2,1)S(1)} %copy-done, bf16[112,1280]{1,0:T(8,128)(2,1)S(1)} %get-tuple-element.28.own_ref.own1_ref, bf16[112,1280]{1,0:T(8,128)(2,1)S(1)} %collective-permute-done.other_ref.other1_ref, bf16[112,1280]{1,0:T(8,128)(2,1)S(1)} %mlp.1.own2_ref, ...), custom_call_target="tpu_custom_call" | custom-call | tf_op jit(solution)/shard_map/head/pallas_call | solution.py:288
  (22 shorter events, 0.1 us)
Async XLA Ops:
  6.5 31.7 %copy-start.16 = (s32[480]{0:T(512)S(1)}, s32[480]{0:T(512)}, u32[]{:S(2)}) copy-start(s32[480]{0:T(512)} %constant.44.clone) | copy-start | bytes 5764
  6.5 123.8 %all-gather.3.cloned.1.call-start = ((), (), s32[]{:S(2)}) async-start(), calls=%async_computation.5 | async-start | bytes 10444800 | tf_op jit(solution)/shard_map/all_gather | solution.py:349
  26.6 13.2 %copy-start.4 = (bf16[2,640,5]{1,0,2:T(2,128)(2,1)S(1)}, bf16[2,640,5]{1,0,2:T(2,128)(2,1)}, u32[]{:S(2)}) copy-start(bf16[2,640,5]{1,0,2:T(2,128)(2,1)} %param.32) | copy-start | bytes 38404
  26.6 13.2 %copy-start.5 = (bf16[5,640]{1,0:T(8,128)(2,1)S(1)}, bf16[5,640]{1,0:T(8,128)(2,1)}, u32[]{:S(2)}) copy-start(bf16[5,640]{1,0:T(8,128)(2,1)} %param.31) | copy-start | bytes 19204
  26.6 23.1 %copy-start.10 = (s32[320]{0:T(512)S(1)}, s32[320]{0:T(512)}, u32[]{:S(2)}) copy-start(s32[320]{0:T(512)} %constant.50.clone) | copy-start | bytes 3844
  26.6 23.2 %copy-start.11 = (s32[160]{0:T(256)S(1)}, s32[160]{0:T(256)}, u32[]{:S(2)}) copy-start(s32[160]{0:T(256)} %constant.47.clone) | copy-start | bytes 1924
  26.6 23.2 %copy-start.12 = (s32[160]{0:T(256)S(1)}, s32[160]{0:T(256)}, u32[]{:S(2)}) copy-start(s32[160]{0:T(256)} %constant.46.clone) | copy-start | bytes 1924
  26.7 23.2 %copy-start.9 = (s32[640]{0:T(1024)S(1)}, s32[640]{0:T(1024)}, u32[]{:S(2)}) copy-start(s32[640]{0:T(1024)} %constant.49.clone) | copy-start | bytes 7684
  26.7 23.2 %copy-start.14 = (f32[80]{0:T(128)S(1)}, f32[80]{0:T(128)}, u32[]{:S(2)}) copy-start(f32[80]{0:T(128)} %param.26) | copy-start | bytes 964
  26.7 23.3 %copy-start.8 = (f32[1280]{0:T(1024)S(1)}, f32[1280]{0:T(1024)}, u32[]{:S(2)}) copy-start(f32[1280]{0:T(1024)} %param.25) | copy-start | bytes 15364
  40.6 19.3 %all-to-all-start.2 = ((bf16[16,16,640]{2,1,0:T(8,128)(2,1)}), bf16[16,16,640]{2,1,0:T(8,128)(2,1)S(1)}, u32[]{:S(2)}, u32[]{:S(2)}) async-start(bf16[16,16,640]{2,1,0:T(8,128)(2,1)} %broadcast_in_dim.14), calls=%async_computation.2 | async-start | bytes 655360 | tf_op jit(solution)/shard_map/all_to_all | solution.py:88
  50.3 14.4 %copy-start.3 = (bf16[112,1280]{1,0:T(8,128)(2,1)S(1)}, bf16[112,1280]{1,0:T(8,128)(2,1)}, u32[]{:S(2)}) copy-start(bf16[112,1280]{1,0:T(8,128)(2,1)} %param.20) | copy-start | bytes 860164
  50.3 14.5 %copy-start.6 = (f32[1280]{0:T(1024)S(1)}, f32[1280]{0:T(1024)}, u32[]{:S(2)}) copy-start(f32[1280]{0:T(1024)} %param.24) | copy-start | bytes 15364
  50.8 14.2 %copy-start.7 = (s32[1280]{0:T(1024)S(1)}, s32[1280]{0:T(1024)}, u32[]{:S(2)}) copy-start(s32[1280]{0:T(1024)} %constant.45.clone) | copy-start | bytes 15364
  61.2 17.4 %all-to-all-start.3 = ((bf16[4,160,640]{2,1,0:T(8,128)(2,1)}), bf16[4,160,640]{2,1,0:T(8,128)(2,1)S(1)}, u32[]{:S(2)}, u32[]{:S(2)}) async-start(bf16[4,160,640]{2,1,0:T(8,128)(2,1)} %broadcast_in_dim.16), calls=%async_computation.3 | async-start | bytes 1638400 | tf_op jit(solution)/shard_map/all_to_all | solution.py:88
  67.4 11.2 %copy-start.15 = (s32[640]{0:T(1024)S(1)}, s32[640]{0:T(1024)}, u32[]{:S(2)}) copy-start(s32[640]{0:T(1024)} %constant.48.clone) | copy-start | bytes 7684
  71.0 8.5 %copy-start.13 = (s32[112]{0:T(128)S(1)}, s32[112]{0:T(128)}, u32[]{:S(2)}) copy-start(s32[112]{0:T(128)} %param.23) | copy-start | bytes 1348
  125.2 29.2 %collective-permute-start.2 = (bf16[4,640,640]{2,1,0:T(8,128)(2,1)}, bf16[4,640,640]{2,1,0:T(8,128)(2,1)S(1)}, u32[]{:S(2)}, u32[]{:S(2)}) collective-permute-start(bf16[4,640,640]{2,1,0:T(8,128)(2,1)} %all_to_all.27.near_hbm), channel_id=1, source_target_pairs={{0,2},{2,0},{1,3},{3,1},{4,6},{6,4},{5,7},{7,5},{8,10},{10,8},{9,1... | collective-permute-start | bytes 9830408 | tf_op jit(solution)/shard_map/ppermute | solution.py:382
  130.3 1.6 copy-start.1
  132.0 1.0 copy-start.2
  132.9 17.9 %copy-start = (bf16[112,1280]{1,0:T(8,128)(2,1)S(1)}, bf16[112,1280]{1,0:T(8,128)(2,1)}, u32[]{:S(2)}) copy-start(bf16[112,1280]{1,0:T(8,128)(2,1)} %get-tuple-element.23.stream_ref) | copy-start | bytes 860164
  140.6 10.3 %collective-permute-start = (bf16[112,1280]{1,0:T(8,128)(2,1)S(1)}, bf16[112,1280]{1,0:T(8,128)(2,1)S(1)}, u32[]{:S(2)}, u32[]{:S(2)}) collective-permute-start(bf16[112,1280]{1,0:T(8,128)(2,1)S(1)} %get-tuple-element.28.own_ref.own1_ref), channel_id=1, source_target_pairs={{0,1},{1,0},{2,3},{3,2},{4,5},{5,4},{6,7},{7,6},{8,9},{9,8},{10,11... | collective-permute-start | bytes 860168 | tf_op jit(solution)/shard_map/ppermute | solution.py:314
  152.0 9.4 %collective-permute-start.1 = (bf16[112,1280]{1,0:T(8,128)(2,1)S(1)}, bf16[112,1280]{1,0:T(8,128)(2,1)S(1)}, u32[]{:S(2)}, u32[]{:S(2)}) collective-permute-start(bf16[112,1280]{1,0:T(8,128)(2,1)S(1)} %mlp.1.own2_ref), channel_id=1, source_target_pairs={{0,1},{1,0},{2,3},{3,2},{4,5},{5,4},{6,7},{7,6},{8,9},{9,8},{10,11... | collective-permute-start | bytes 860168 | tf_op jit(solution)/shard_map/ppermute | solution.py:314
Sparse Core Ops, SparseCore 0:
  39.9 69.2 all-gather.2

commit v4 on v3

--- a/solution.py
+++ b/solution.py
@@ -219,56 +219,84 @@
     )(stream, own, other, gain, in_vmem(w))
 
 
-def head_body(
-    stream_ref, own1_ref, other1_ref, own2_ref, other2_ref, far_ref,
-    turn_hbm, plain_hbm, last_hbm, near_hbm,
-    out_ref, turn_buf, plain_buf, last_buf, near_ref, sems,
+def part(ref, start, count):
+    return ref[:, pl.ds(start, count), :].reshape(NX * count, ref.shape[-1])
+
+
+def near_head_body(
+    stream_ref, own1_ref, other1_ref, own2_ref, other2_ref, turn_hbm, plain_hbm, near_hbm,
+    rest_ref, skip_ref, pre0_ref, pre1_ref, turn_ref, plain_ref, near_ref, sems,
 ):
-    width = near_ref.shape[-1]
     half = D // NC
     each = half // NX
-    rows = 2 * each
-    load_turn = pltpu.make_async_copy(turn_hbm, turn_buf, sems.at[0])
-    load_plain = pltpu.make_async_copy(plain_hbm, plain_buf, sems.at[1])
-    load_last = pltpu.make_async_copy(last_hbm, last_buf, sems.at[2])
-    loads = [
-        pltpu.make_async_copy(
-            near_hbm.at[:, pl.ds(n * rows, rows), :],
-            near_ref.at[:, pl.ds(n * rows, rows), :],
-            sems.at[3 + n],
-        )
-        for n in range(2)
-    ]
+    load_turn = pltpu.make_async_copy(turn_hbm, turn_ref, sems.at[0])
+    load_near = pltpu.make_async_copy(near_hbm.at[:, pl.ds(0, 2 * each), :], near_ref, sems.at[1])
+    load_plain = pltpu.make_async_copy(plain_hbm, plain_ref, sems.at[2])
     load_turn.start()
-    loads[0].start()
-
-    def part(ref, start, count):
-        return ref[:, pl.ds(start, count), :].reshape(NX * count, width)
-
+    load_near.start()
     s1 = stream_ref[...].astype(F32) + (own1_ref[...].astype(F32) + other1_ref[...].astype(F32))
     s2 = (s1 + (own2_ref[...].astype(F32) + other2_ref[...].astype(F32))).astype(BF16)
     load_turn.wait()
     load_plain.start()
-    loads[1].start()
+    turned = dot(s2, turn_ref[...]).astype(BF16)
+    rest_ref[...] = turned[:, half:]
+    load_near.wait()
+    pre0_ref[...] = dot(turned[:, :half], part(near_ref, 0, each))
+    pre1_ref[...] = dot(turned[:, :half], part(near_ref, each, each))
+    load_plain.wait()
+    skip_ref[...] = dot(s2, plain_ref[...]).astype(BF16)
+
+
+def near_head_kernel(stream, own1, other1, own2, other2, turn, plain, near):
+    rows = stream.shape[0]
+    width = near.shape[-1]
+    vmem = pl.BlockSpec(memory_space=pltpu.VMEM)
+    return pl.pallas_call(
+        near_head_body,
+        out_shape=(
+            pltpu.VMEM((rows, D // NC), BF16),
+            pltpu.VMEM((rows, D), BF16),
+            pltpu.VMEM((rows, width), F32),
+            pltpu.VMEM((rows, width), F32),
+        ),
+        in_specs=[vmem] * 5 + [pl.BlockSpec(memory_space=pltpu.HBM)] * 3,
+        out_specs=(vmem,) * 4,
+        scratch_shapes=[
+            pltpu.VMEM(turn.shape, BF16),
+            pltpu.VMEM(plain.shape, BF16),
+            pltpu.VMEM((NX, near.shape[1] // 2, width), BF16),
+            pltpu.SemaphoreType.DMA((3,)),
+        ],
+        compiler_params=pltpu.CompilerParams(vmem_limit_bytes=24 * 2**20),
+        name="near_head",
+    )(stream, own1, other1, own2, other2, in_hbm(turn), in_hbm(plain), in_hbm(near))
+
+
+def head_body(
+    rest_ref, skip_ref, pre0_ref, pre1_ref, far_ref, last_hbm, near_hbm,
+    out_ref, last_buf, near_ref, sems,
+):
+    width = near_ref.shape[-1]
+    each = D // NC // NX
+    load_near = pltpu.make_async_copy(
+        near_hbm.at[:, pl.ds(2 * each, 2 * each), :], near_ref, sems.at[0]
+    )
+    load_last = pltpu.make_async_copy(last_hbm, last_buf, sems.at[1])
+    load_near.start()
     load_last.start()
-    turned = dot(s2, turn_buf[...]).astype(BF16)
-    loads[0].wait()
-
-    def hidden(start):
-        pre = dot(turned[:, :half], part(near_ref, start, each))
-        pre = pre + dot(turned[:, half:], part(far_ref, start, each))
+
+    def hidden(pre_ref, start):
+        pre = pre_ref[...] + dot(rest_ref[...], part(far_ref, start, each))
         return (pre / (1.0 + jnp.exp(-pre))).astype(BF16)
 
-    act = (hidden(0), hidden(each))
-    load_plain.wait()
-    plain = dot(s2, plain_buf[...]).astype(BF16)
-    skip = (plain[:, :width], plain[:, width:])
-    loads[1].wait()
+    act = (hidden(pre0_ref, 0), hidden(pre1_ref, each))
+    skip = (skip_ref[:, :width], skip_ref[:, width:])
+    load_near.wait()
     out = []
-    for ref in (near_ref, far_ref):
+    for ref, start in ((near_ref, 0), (far_ref, 2 * each)):
         total = None
         for k in range(2):
-            at = 2 * each + k * (each // 2)
+            at = start + k * (each // 2)
             term = dot_t(act[k], part(ref, at, each // 2))
             term = term + dot_t(skip[k], part(ref, at + each, each // 2))
             total = term if total is None else total + term
@@ -280,29 +308,24 @@
     out_ref[...] = dot(high, last_buf[...]) + dot(low, last_buf[...])
 
 
-def head_kernel(stream, own1, other1, own2, other2, turn, plain, last, near, far):
-    rows = stream.shape[0]
+def head_kernel(rest, skip, pre0, pre1, far, last, near):
+    rows = rest.shape[0]
     width = near.shape[-1]
     vmem = pl.BlockSpec(memory_space=pltpu.VMEM)
     hbm = pl.BlockSpec(memory_space=pltpu.HBM)
     return pl.pallas_call(
         head_body,
         out_shape=jax.ShapeDtypeStruct((rows, width), F32),
-        in_specs=[vmem] * 6 + [hbm] * 4,
+        in_specs=[vmem] * 5 + [hbm] * 2,
         out_specs=vmem,
         scratch_shapes=[
-            pltpu.VMEM(turn.shape, BF16),
-            pltpu.VMEM(plain.shape, BF16),
             pltpu.VMEM(last.shape, BF16),
-            pltpu.VMEM(near.shape, BF16),
-            pltpu.SemaphoreType.DMA((5,)),
+            pltpu.VMEM((NX, near.shape[1] // 2, width), BF16),
+            pltpu.SemaphoreType.DMA((2,)),
         ],
-        compiler_params=pltpu.CompilerParams(vmem_limit_bytes=32 * 2**20),
+        compiler_params=pltpu.CompilerParams(vmem_limit_bytes=12 * 2**20),
         name="head",
-    )(
-        stream, own1, other1, own2, other2, in_vmem(far),
-        in_hbm(turn), in_hbm(plain), in_hbm(last), in_hbm(near),
-    )
+    )(rest, skip, pre0, pre1, in_vmem(far), in_hbm(last), in_hbm(near))
 
 
 def rms_scale(values, gain):
@@ -387,9 +410,10 @@
     other1 = swap(part1)
     part2 = mlp_kernel(stream_o, part1, other1, gain_o, feed_w)
     other2 = swap(part2)
-    return head_kernel(
-        stream_o, part1, other1, part2, other2, turn, plain, last, near, far
-    )
+    rest, skip, pre0, pre1 = near_head_kernel(
+        stream_o, part1, other1, part2, other2, turn, plain, near
+    )
+    return head_kernel(rest, skip, pre0, pre1, far, last, near)
 
 
 def solution(mesh):

time: 177 us -> 179 us (1.011)
  Pallas kernels: 16.4 us -> 18.2 us
    pallas_call x0 -> x1, Pallas kernels: none -> 4.67 us  [near_head_kernel(): pl.pallas_call(near_head_body, out_shape=(pltpu.VMEM((rows, D // NC), BF1...]
    pallas_call x1, Pallas kernels: 7.67 us -> 4.76 us  [head_kernel(): pl.pallas_call(head_body, out_shape=jax.ShapeDtypeStruct((rows, width), F...]
  transfers between devices with their start and end apart: 6 -> 6, of which waited for: 4 -> 4; matrix products, arithmetic and copies ran while one was open for 7% -> 6% of each run, Pallas kernels for 5% -> 8%
where the time goes in v4:
time: 179 us; the launch traced here: 178 us
  blocking collectives  75.3 us (42%)
  waiting for transfers between devices  31.1 us (17%)
  starting transfers between devices  22.1 us (12%)
  Pallas kernels  18.2 us (10%)
  between operations  13.8 us (8%)
  local copies, waits for them, and re-layouts  7.04 us (4%)
  other arithmetic  6.02 us (3%)
  matrix products  4.16 us (2%)
    all_to_all x3, blocking collectives, from_all(): return lax.all_to_all(copies, axis, split_axis=0, concat_axis=0, tiled=True)  75.3 us
    all_to_all x2, waiting for transfers between devices, from_all(): return lax.all_to_all(copies, axis, split_axis=0, concat_axis=0, tiled=True)  15.7 us
    ppermute x2, waiting for transfers between devices, swap(): return lax.ppermute(array, 'mp', [(0, 1), (1, 0)])  15.4 us
    all_to_all x2, starting transfers between devices, from_all(): return lax.all_to_all(copies, axis, split_axis=0, concat_axis=0, tiled=True)  12.7 us
    pallas_call x1, Pallas kernels, attention_kernel(): pl.pallas_call(attention_body, out_shape=(pltpu.VMEM((rows, D), BF16), pl...  7.66 us
    ppermute x1, starting transfers between devices, per_device(): far = lax.ppermute(near, 'c', [(0, 1), (1, 0)])  5.12 us
    pallas_call x1, Pallas kernels, head_kernel(): pl.pallas_call(head_body, out_shape=jax.ShapeDtypeStruct((rows, width), F...  4.76 us
    pallas_call x1, Pallas kernels, near_head_kernel(): pl.pallas_call(near_head_body, out_shape=(pltpu.VMEM((rows, D // NC), BF1...  4.67 us
  transfers between devices with their start and end apart: 6, of which 4 were waited for; matrix products, arithmetic and copies ran while one was open for 6% of the time, Pallas kernels for 8%

profile of v4, /device:TPU:1, one launch (start us, length us, event | category | flops | bytes accessed | tf_op | source)
XLA Modules:
  0.0 177.7 jit_solution(6724090850231373287)
XLA Ops:
  6.5 0.0 all-gather.3.cloned.1.call-start
  6.5 0.8 reshape.66
  7.3 0.8 fusion.22
  8.1 18.5 %all_to_all.25 = bf16[4,32,640]{2,1,0:T(8,128)(2,1)S(1)} all-to-all(bf16[4,32,640]{2,1,0:T(8,128)(2,1)S(1)} %broadcast_in_dim.12), channel_id=1, replica_groups=mesh['y'=8,'zh'=4,'x'=4,'c'=2,'mp'=2] {'zh'}, dimensions={0} | all-to-all | bytes 327680 | tf_op jit(solution)/shard_map/all_to_all | solution.py:88
  26.6 0.1 broadcast_in_dim.13
  26.6 0.0 copy-start.10
  26.6 0.0 copy-start.11
  26.6 0.0 copy-start.12
  26.7 0.0 copy-start.9
  26.7 0.0 copy-start.14
  26.7 0.0 copy-start.8
  26.7 11.6 %all_to_all.26 = bf16[4,128,640]{2,1,0:T(8,128)(2,1)S(1)} all-to-all(bf16[4,128,640]{2,1,0:T(8,128)(2,1)S(1)} %broadcast_in_dim.13), channel_id=1, replica_groups=mesh['y'=8,'zh'=4,'x'=4,'c'=2,'mp'=2] {'x'}, dimensions={0} | all-to-all | bytes 1310720 | tf_op jit(solution)/shard_map/all_to_all | solution.py:88
  38.3 0.0 copy-done.16
  38.3 1.4 convolution_convert_fusion
  39.7 0.0 all-gather.3.cloned.1.call-update
  39.8 0.0 copy-done.4
  39.8 0.0 copy-done.5
  39.8 0.8 broadcast_in_dim.14
  40.6 9.2 %all-to-all-start.2 = ((bf16[16,16,640]{2,1,0:T(8,128)(2,1)}), bf16[16,16,640]{2,1,0:T(8,128)(2,1)S(1)}, u32[]{:S(2)}, u32[]{:S(2)}) async-start(bf16[16,16,640]{2,1,0:T(8,128)(2,1)} %broadcast_in_dim.14), calls=%async_computation.2 | async-start | bytes 655360 | tf_op jit(solution)/shard_map/all_to_all | solution.py:88
  49.8 0.0 copy-done.10
  49.8 0.1 iota_add_fusion
  49.9 0.0 copy-done.11
  49.9 0.0 copy-done.12
  49.9 0.0 copy-done.9
  49.9 0.1 reshape_tile.3.scale_ref
  50.0 0.0 copy-done.8
  50.0 0.3 reshape.71
  50.3 0.0 copy-start.3
  50.3 0.0 copy-start.6
  50.4 0.2 reshape.72.gain_ref
  50.6 0.1 fusion.14.pool_ref
  50.8 0.0 copy-start.7
  50.8 1.1 compare_convert_fusion.1.last_hbm
  51.9 8.1 %all-to-all-done.2 = bf16[16,16,640]{2,1,0:T(8,128)(2,1)S(1)} async-done(((bf16[16,16,640]{2,1,0:T(8,128)(2,1)}), bf16[16,16,640]{2,1,0:T(8,128)(2,1)S(1)}, u32[]{:S(2)}, u32[]{:S(2)}) %all-to-all-start.2) | async-done | bytes 327712 | tf_op jit(solution)/shard_map/all_to_all | solution.py:88
  59.9 0.3 convolution_convert_fusion.1
  60.2 1.0 broadcast_in_dim.16
  61.2 3.5 %all-to-all-start.3 = ((bf16[4,160,640]{2,1,0:T(8,128)(2,1)}), bf16[4,160,640]{2,1,0:T(8,128)(2,1)S(1)}, u32[]{:S(2)}, u32[]{:S(2)}) async-start(bf16[4,160,640]{2,1,0:T(8,128)(2,1)} %broadcast_in_dim.16), calls=%async_computation.3 | async-start | bytes 1638400 | tf_op jit(solution)/shard_map/all_to_all | solution.py:88
  64.7 0.0 copy-done.3
  64.7 0.1 fusion.7
  64.8 0.1 fusion.9
  65.0 0.0 copy-done.7
  65.0 1.5 fusion.3
  66.5 0.9 fusion.30
  67.4 3.6 %fusion.1 = (bf16[1280,1280]{1,0:T(8,128)(2,1)}, bf16[1280,1280]{1,0:T(8,128)(2,1)}) fusion(s32[1280]{0:T(1024)S(1)} %copy-done.7, s32[1280]{0:T(1024)S(1)} %pad_add_fusion), kind=kLoop, calls=%fused_computation.3 | loop fusion | flops 6553600 | bytes 6563840 | tf_op jit(solution)/shard_map/convert_element_type | solution.py:389
  71.0 7.6 %all-to-all-done.3 = bf16[4,160,640]{2,1,0:T(8,128)(2,1)S(1)} async-done(((bf16[4,160,640]{2,1,0:T(8,128)(2,1)}), bf16[4,160,640]{2,1,0:T(8,128)(2,1)S(1)}, u32[]{:S(2)}, u32[]{:S(2)}) %all-to-all-start.3) | async-done | bytes 819232 | tf_op jit(solution)/shard_map/all_to_all | solution.py:88
  78.6 0.0 copy-done.15
  78.6 0.9 fusion.5
  79.5 0.1 broadcast_in_dim.15.valid_ref
  79.6 0.3 broadcast_in_dim.17
  79.9 45.3 %all_to_all.27.near_hbm = bf16[4,640,640]{2,1,0:T(8,128)(2,1)} all-to-all(bf16[4,640,640]{2,1,0:T(8,128)(2,1)S(1)} %broadcast_in_dim.17), channel_id=1, replica_groups=mesh['y'=8,'zh'=4,'x'=4,'c'=2,'mp'=2] {'x'}, dimensions={0} | all-to-all | bytes 6553600 | tf_op jit(solution)/shard_map/all_to_all | solution.py:88
  125.1 5.1 %collective-permute-start.2 = (bf16[4,640,640]{2,1,0:T(8,128)(2,1)}, bf16[4,640,640]{2,1,0:T(8,128)(2,1)S(1)}, u32[]{:S(2)}, u32[]{:S(2)}) collective-permute-start(bf16[4,640,640]{2,1,0:T(8,128)(2,1)} %all_to_all.27.near_hbm), channel_id=1, source_target_pairs={{0,2},{2,0},{1,3},{3,1},{4,6},{6,4},{5,7},{7,5},{8,10},{10,8},{9,1... | collective-permute-start | bytes 9830408 | tf_op jit(solution)/shard_map/ppermute | solution.py:405
  130.3 0.0 all-gather.3.cloned.1.call-done
  130.3 0.0 copy-start.1
  130.3 1.6 copy-done.1
  131.9 1.0 copy-done.2
  132.9 7.7 %attend.1 = (bf16[112,1280]{1,0:T(8,128)(2,1)S(1)}, bf16[2,16,80,640]{3,2,1,0:T(8,128)(2,1)S(1)}) custom-call(bf16[112,1280]{1,0:T(8,128)(2,1)S(1)} %copy-done.2, f32[1,640]{1,0:T(1,128)S(1)} %reshape_tile.3.scale_ref, s32[112,128]{1,0:T(8,128)S(1)} %broadcast_in_dim.15.valid_ref, bf16[640,128]{1,0:T(8,128)(2,1)S(1)} %fusion.14.pool_ref, ...), custom_call_target="tpu_custom_call" | custom-call | tf_op jit(solution)/shard_map/attend/pallas_call | solution.py:181
  140.6 1.9 %collective-permute-start = (bf16[112,1280]{1,0:T(8,128)(2,1)S(1)}, bf16[112,1280]{1,0:T(8,128)(2,1)S(1)}, u32[]{:S(2)}, u32[]{:S(2)}) collective-permute-start(bf16[112,1280]{1,0:T(8,128)(2,1)S(1)} %get-tuple-element.32.own_ref.own1_ref), channel_id=1, source_target_pairs={{0,1},{1,0},{2,3},{3,2},{4,5},{5,4},{6,7},{7,6},{8,9},{9,8},{10,11... | collective-permute-start | bytes 860168 | tf_op jit(solution)/shard_map/ppermute | solution.py:337
  142.5 8.3 %collective-permute-done.other_ref.other1_ref = bf16[112,1280]{1,0:T(8,128)(2,1)S(1)} collective-permute-done((bf16[112,1280]{1,0:T(8,128)(2,1)S(1)}, bf16[112,1280]{1,0:T(8,128)(2,1)S(1)}, u32[]{:S(2)}, u32[]{:S(2)}) %collective-permute-start) | collective-permute-done | bytes 286752 | tf_op jit(solution)/shard_map/ppermute | solution.py:337
  150.8 1.1 mlp.1.own2_ref
  152.0 2.4 %collective-permute-start.1 = (bf16[112,1280]{1,0:T(8,128)(2,1)S(1)}, bf16[112,1280]{1,0:T(8,128)(2,1)S(1)}, u32[]{:S(2)}, u32[]{:S(2)}) collective-permute-start(bf16[112,1280]{1,0:T(8,128)(2,1)S(1)} %mlp.1.own2_ref), channel_id=1, source_target_pairs={{0,1},{1,0},{2,3},{3,2},{4,5},{5,4},{6,7},{7,6},{8,9},{9,8},{10,11... | collective-permute-start | bytes 860168 | tf_op jit(solution)/shard_map/ppermute | solution.py:337
  154.4 7.0 %collective-permute-done.1.other2_ref = bf16[112,1280]{1,0:T(8,128)(2,1)S(1)} collective-permute-done((bf16[112,1280]{1,0:T(8,128)(2,1)S(1)}, bf16[112,1280]{1,0:T(8,128)(2,1)S(1)}, u32[]{:S(2)}, u32[]{:S(2)}) %collective-permute-start.1) | collective-permute-done | bytes 286752 | tf_op jit(solution)/shard_map/ppermute | solution.py:337
  161.4 4.7 %near_head.1 = (bf16[112,640]{1,0:T(8,128)(2,1)S(1)}, bf16[112,1280]{1,0:T(8,128)(2,1)S(1)}, f32[112,640]{1,0:T(8,128)S(1)}, f32[112,640]{1,0:T(8,128)S(1)}) custom-call(bf16[112,1280]{1,0:T(8,128)(2,1)S(1)} %copy-done, bf16[112,1280]{1,0:T(8,128)(2,1)S(1)} %get-tuple-element.32.own_ref.own1_ref, ...), custom_call_target="tpu_custom_call" | custom-call | tf_op jit(solution)/shard_map/near_head/pallas_call | solution.py:254
  166.1 0.0 collective-permute-done.2.far_ref
  166.1 4.8 %head.1 = f32[112,640]{1,0:T(8,128)} custom-call(bf16[112,640]{1,0:T(8,128)(2,1)S(1)} %get-tuple-element.38.rest_ref, bf16[112,1280]{1,0:T(8,128)(2,1)S(1)} %get-tuple-element.39.skip_ref, f32[112,640]{1,0:T(8,128)S(1)} %get-tuple-element.40.pre0_ref, f32[112,640]{1,0:T(8,128)S(1)} %get-tuple-element.41.pre1_ref, ...), custom_call_target="tpu_custom_call" | custom-call | tf_op jit(solution)/shard_map/head/pallas_call | solution.py:316
  (23 shorter events, 0.1 us)
Async XLA Ops:
  6.5 31.7 %copy-start.16 = (s32[480]{0:T(512)S(1)}, s32[480]{0:T(512)}, u32[]{:S(2)}) copy-start(s32[480]{0:T(512)} %constant.44.clone) | copy-start | bytes 5764
  6.5 123.7 %all-gather.3.cloned.1.call-start = ((), (), s32[]{:S(2)}) async-start(), calls=%async_computation.5 | async-start | bytes 10444800 | tf_op jit(solution)/shard_map/all_gather | solution.py:372
  26.6 13.2 %copy-start.4 = (bf16[2,640,5]{1,0,2:T(2,128)(2,1)S(1)}, bf16[2,640,5]{1,0,2:T(2,128)(2,1)}, u32[]{:S(2)}) copy-start(bf16[2,640,5]{1,0,2:T(2,128)(2,1)} %param.32) | copy-start | bytes 38404
  26.6 13.2 %copy-start.5 = (bf16[5,640]{1,0:T(8,128)(2,1)S(1)}, bf16[5,640]{1,0:T(8,128)(2,1)}, u32[]{:S(2)}) copy-start(bf16[5,640]{1,0:T(8,128)(2,1)} %param.31) | copy-start | bytes 19204
  26.6 23.1 %copy-start.10 = (s32[320]{0:T(512)S(1)}, s32[320]{0:T(512)}, u32[]{:S(2)}) copy-start(s32[320]{0:T(512)} %constant.50.clone) | copy-start | bytes 3844
  26.6 23.2 %copy-start.11 = (s32[160]{0:T(256)S(1)}, s32[160]{0:T(256)}, u32[]{:S(2)}) copy-start(s32[160]{0:T(256)} %constant.47.clone) | copy-start | bytes 1924
  26.6 23.2 %copy-start.12 = (s32[160]{0:T(256)S(1)}, s32[160]{0:T(256)}, u32[]{:S(2)}) copy-start(s32[160]{0:T(256)} %constant.46.clone) | copy-start | bytes 1924
  26.7 23.2 %copy-start.9 = (s32[640]{0:T(1024)S(1)}, s32[640]{0:T(1024)}, u32[]{:S(2)}) copy-start(s32[640]{0:T(1024)} %constant.49.clone) | copy-start | bytes 7684
  26.7 23.2 %copy-start.14 = (f32[80]{0:T(128)S(1)}, f32[80]{0:T(128)}, u32[]{:S(2)}) copy-start(f32[80]{0:T(128)} %param.26) | copy-start | bytes 964
  26.7 23.3 %copy-start.8 = (f32[1280]{0:T(1024)S(1)}, f32[1280]{0:T(1024)}, u32[]{:S(2)}) copy-start(f32[1280]{0:T(1024)} %param.25) | copy-start | bytes 15364
  40.6 19.4 %all-to-all-start.2 = ((bf16[16,16,640]{2,1,0:T(8,128)(2,1)}), bf16[16,16,640]{2,1,0:T(8,128)(2,1)S(1)}, u32[]{:S(2)}, u32[]{:S(2)}) async-start(bf16[16,16,640]{2,1,0:T(8,128)(2,1)} %broadcast_in_dim.14), calls=%async_computation.2 | async-start | bytes 655360 | tf_op jit(solution)/shard_map/all_to_all | solution.py:88
  50.3 14.4 %copy-start.3 = (bf16[112,1280]{1,0:T(8,128)(2,1)S(1)}, bf16[112,1280]{1,0:T(8,128)(2,1)}, u32[]{:S(2)}) copy-start(bf16[112,1280]{1,0:T(8,128)(2,1)} %param.20) | copy-start | bytes 860164
  50.3 14.5 %copy-start.6 = (f32[1280]{0:T(1024)S(1)}, f32[1280]{0:T(1024)}, u32[]{:S(2)}) copy-start(f32[1280]{0:T(1024)} %param.24) | copy-start | bytes 15364
  50.8 14.2 %copy-start.7 = (s32[1280]{0:T(1024)S(1)}, s32[1280]{0:T(1024)}, u32[]{:S(2)}) copy-start(s32[1280]{0:T(1024)} %constant.45.clone) | copy-start | bytes 15364
  61.2 17.4 %all-to-all-start.3 = ((bf16[4,160,640]{2,1,0:T(8,128)(2,1)}), bf16[4,160,640]{2,1,0:T(8,128)(2,1)S(1)}, u32[]{:S(2)}, u32[]{:S(2)}) async-start(bf16[4,160,640]{2,1,0:T(8,128)(2,1)} %broadcast_in_dim.16), calls=%async_computation.3 | async-start | bytes 1638400 | tf_op jit(solution)/shard_map/all_to_all | solution.py:88
  67.4 11.2 %copy-start.15 = (s32[640]{0:T(1024)S(1)}, s32[640]{0:T(1024)}, u32[]{:S(2)}) copy-start(s32[640]{0:T(1024)} %constant.48.clone) | copy-start | bytes 7684
  70.9 8.6 %copy-start.13 = (s32[112]{0:T(128)S(1)}, s32[112]{0:T(128)}, u32[]{:S(2)}) copy-start(s32[112]{0:T(128)} %param.23) | copy-start | bytes 1348
  125.1 40.9 %collective-permute-start.2 = (bf16[4,640,640]{2,1,0:T(8,128)(2,1)}, bf16[4,640,640]{2,1,0:T(8,128)(2,1)S(1)}, u32[]{:S(2)}, u32[]{:S(2)}) collective-permute-start(bf16[4,640,640]{2,1,0:T(8,128)(2,1)} %all_to_all.27.near_hbm), channel_id=1, source_target_pairs={{0,2},{2,0},{1,3},{3,1},{4,6},{6,4},{5,7},{7,5},{8,10},{10,8},{9,1... | collective-permute-start | bytes 9830408 | tf_op jit(solution)/shard_map/ppermute | solution.py:405
  130.3 1.6 copy-start.1
  131.9 1.0 copy-start.2
  132.9 17.9 %copy-start = (bf16[112,1280]{1,0:T(8,128)(2,1)S(1)}, bf16[112,1280]{1,0:T(8,128)(2,1)}, u32[]{:S(2)}) copy-start(bf16[112,1280]{1,0:T(8,128)(2,1)} %get-tuple-element.27.stream_ref) | copy-start | bytes 860164
  140.6 10.3 %collective-permute-start = (bf16[112,1280]{1,0:T(8,128)(2,1)S(1)}, bf16[112,1280]{1,0:T(8,128)(2,1)S(1)}, u32[]{:S(2)}, u32[]{:S(2)}) collective-permute-start(bf16[112,1280]{1,0:T(8,128)(2,1)S(1)} %get-tuple-element.32.own_ref.own1_ref), channel_id=1, source_target_pairs={{0,1},{1,0},{2,3},{3,2},{4,5},{5,4},{6,7},{7,6},{8,9},{9,8},{10,11... | collective-permute-start | bytes 860168 | tf_op jit(solution)/shard_map/ppermute | solution.py:337
  152.0 9.4 %collective-permute-start.1 = (bf16[112,1280]{1,0:T(8,128)(2,1)S(1)}, bf16[112,1280]{1,0:T(8,128)(2,1)S(1)}, u32[]{:S(2)}, u32[]{:S(2)}) collective-permute-start(bf16[112,1280]{1,0:T(8,128)(2,1)S(1)} %mlp.1.own2_ref), channel_id=1, source_target_pairs={{0,1},{1,0},{2,3},{3,2},{4,5},{5,4},{6,7},{7,6},{8,9},{9,8},{10,11... | collective-permute-start | bytes 860168 | tf_op jit(solution)/shard_map/ppermute | solution.py:337
Sparse Core Ops, SparseCore 0:
  39.9 69.2 all-gather.2
